TPU v7x, 32 devices: a whole 2x2x4 slice. The times are simulated.
32 devices in a mesh: seq: 4 (over x, core), head: 8 (over z, y).
Axes of the slice: x: 2, y: 2, z: 4, core: 2. Of those that a mesh axis runs over, the one named last changes fastest.
Arguments:
- residual_in: float32 [1, 4096, 1536], P(None, ('seq', 'head')), may hold values from -6 to 6
- norm_gain: float32 [1536], replicated, may hold values from 0.5 to 1.5
- gate_weight: float32 [3072, 1536], P('head'), may hold values from -0.15625 to 0.15625
- inner_weight: float32 [3072, 1536], P('head'), may hold values from -0.15625 to 0.15625
- bc_weight: float32 [1536, 256], replicated, may hold values from -0.15625 to 0.15625
- step_weight: float32 [48, 1536], P('head'), may hold values from -0.15625 to 0.15625
- conv_inner_weight: float32 [4, 3072], P(None, 'head'), may hold values from -3 to 3
- conv_inner_bias: float32 [3072], P('head'), may hold values from -0.5 to 0.5
- conv_bc_weight: float32 [4, 256], replicated, may hold values from -3 to 3
- conv_bc_bias: float32 [256], replicated, may hold values from -0.5 to 0.5
- step_bias: float32 [48], P('head'), may hold values from -4 to 0
- decay_log: float32 [48], P('head'), may hold values from -7 to -1
- skip_gain: float32 [48], P('head'), may hold values from 0.5 to 2
- gated_gain: float32 [3072], P('head'), may hold values from 0.5 to 1.5
- out_weight: float32 [3072, 1536], P('head'), may hold values from -0.109375 to 0.109375
- cotangent: float32 [1, 4096, 1536], P(None, ('seq', 'head')), may hold values from -6 to 6
Outputs:
- result: float32 [1, 4096, 1536], P(None, ('seq', 'head'))
- residual_grad: float32 [1, 4096, 1536], P(None, ('seq', 'head'))
- norm_gain_grad: float32 [1536], replicated
- gate_weight_grad: float32 [3072, 1536], P('head')
- inner_weight_grad: float32 [3072, 1536], P('head')
- bc_weight_grad: float32 [1536, 256], replicated
- step_weight_grad: float32 [48, 1536], P('head')
- conv_inner_weight_grad: float32 [4, 3072], P(None, 'head')
- conv_inner_bias_grad: float32 [3072], P('head')
- conv_bc_weight_grad: float32 [4, 256], replicated
- conv_bc_bias_grad: float32 [256], replicated
- step_bias_grad: float32 [48], P('head')
- decay_log_grad: float32 [48], P('head')
- skip_gain_grad: float32 [48], P('head')
- gated_gain_grad: float32 [3072], P('head')
- out_weight_grad: float32 [3072, 1536], P('head')
All inputs are finite; a program needn't handle non-finite values.
Results may differ from a plain program's by a relative error of at most 0.0003.
Values sent between devices are 32-bit elements; how exact they have to be, the bound alone decides.
A program may use at most 192 MiB of HBM per device.

v0:
```python
import jax
import jax.numpy as jnp
from jax import lax
from jax.sharding import PartitionSpec as P

D = 1536
HEADDIM = 64
NSTATE = 128
WIDTH = 4
BLOCK = 256
DI = 3072


EPSILON = 1e-05
HIGH = lax.Precision.HIGHEST


def shifted(value, axis, steps):
    count = lax.axis_size(axis)
    initial, last = (max(0, -steps), min(count, count - steps))
    return lax.ppermute(value, axis, [(source, source + steps) for source in range(initial, last)])


def entering_2(x, axis, combine, identity, reverse):
    devices, here = (lax.axis_size(axis), lax.axis_index(axis))
    everything = jax.tree.map(lambda part: lax.all_gather(part, axis), x)
    start = jax.tree.map(
        lambda part, zero: jnp.broadcast_to(jnp.asarray(zero, part.dtype), part.shape), x, identity
    )

    def step(k, before):
        at = devices - 1 - k if reverse else k
        reached = at > here if reverse else at < here
        new = combine(before, jax.tree.map(lambda part: part[at], everything))
        return jax.tree.map(lambda a, b: jnp.where(reached, a, b), new, before)

    return lax.fori_loop(0, devices, step, start)


def product(left_side, right_side):
    return jnp.dot(left_side, right_side, precision=HIGH, preferred_element_type=jnp.float32)


def product_rows(left_side, right_side):
    return lax.dot_general(
        left_side,
        right_side,
        (((1,), (1,)), ((), ())),
        precision=HIGH,
        preferred_element_type=jnp.float32,
    )


def product_cols(left_side, right_side):
    return lax.dot_general(
        left_side,
        right_side,
        (((0,), (0,)), ((), ())),
        precision=HIGH,
        preferred_element_type=jnp.float32,
    )


def swish_slope(values):
    logistic = jax.nn.sigmoid(values)
    return logistic * (1.0 + values * (1.0 - logistic))


def link_states(earlier, later):
    return (earlier[0] * later[0], later[0][..., None, None] * earlier[1] + later[1])


def block_parts(inner_x, step_size, rate_vec, write_rows):
    batches, local_len, heads_here = step_size.shape
    blocks_here = local_len // BLOCK
    lower = jnp.tril(jnp.ones((BLOCK, BLOCK), jnp.float32))
    log_step = (step_size * rate_vec).reshape(batches, blocks_here, BLOCK, heads_here)
    cumulative = jnp.einsum("ts,bcsh->bcht", lower, log_step, precision=HIGH)
    step_blocks = jnp.swapaxes(step_size.reshape(batches, blocks_here, BLOCK, heads_here), 2, 3)
    tails = jnp.exp(cumulative[..., -1:] - cumulative) * step_blocks
    inner_blocks = inner_x.reshape(batches, blocks_here, BLOCK, heads_here, HEADDIM)
    write_blocks = write_rows.reshape(batches, blocks_here, BLOCK, NSTATE)
    states = jnp.einsum("bchs,bcshp,bcsn->bchpn", tails, inner_blocks, write_blocks, precision=HIGH)
    return (cumulative, states)


def device_summary(cumulative, states):
    totals = cumulative[..., -1]
    carried = jnp.zeros_like(states[:, 0])
    entering = []
    for position in range(states.shape[1]):
        entering.append(carried)
        carried = jnp.exp(totals[:, position])[..., None, None] * carried + states[:, position]
    prefix = jnp.cumsum(totals, axis=1) - totals
    return (carried, jnp.sum(totals, axis=1), jnp.stack(entering, 1), prefix)


def block_output(cumulative, entering, prefix, inner_x, step_size, write_rows, read_rows, state_in):
    batches, local_len, heads_here = step_size.shape
    blocks_here = local_len // BLOCK
    step_blocks = jnp.swapaxes(step_size.reshape(batches, blocks_here, BLOCK, heads_here), 2, 3)
    inner_blocks = inner_x.reshape(batches, blocks_here, BLOCK, heads_here, HEADDIM)
    write_blocks = write_rows.reshape(batches, blocks_here, BLOCK, NSTATE)
    read_blocks = read_rows.reshape(batches, blocks_here, BLOCK, NSTATE)
    start_state = entering + jnp.exp(prefix)[..., None, None] * state_in[:, None]
    causal = jnp.tril(jnp.ones((BLOCK, BLOCK), bool))
    spread = cumulative[..., :, None] - cumulative[..., None, :]
    decay = jnp.where(causal, jnp.exp(jnp.where(causal, spread, 0.0)), 0.0)
    scores = jnp.einsum("bctn,bcsn->bcts", read_blocks, write_blocks, precision=HIGH)
    weights = decay * scores[:, :, None] * step_blocks[:, :, :, None, :]
    intra = jnp.einsum("bchts,bcshp->bcthp", weights, inner_blocks, precision=HIGH)
    carried = (
        jnp.einsum("bctn,bchpn->bchtp", read_blocks, start_state, precision=HIGH)
        * jnp.exp(cumulative)[..., None]
    )
    return (intra + jnp.swapaxes(carried, 2, 3)).reshape(batches, local_len, heads_here, HEADDIM)


def on_device(
    residual_in,
    norm_gain,
    gate_weight,
    inner_weight,
    bc_weight,
    step_weight,
    conv_inner_weight,
    conv_inner_bias,
    conv_bc_weight,
    conv_bc_bias,
    step_bias,
    decay_log,
    skip_gain,
    gated_gain,
    out_weight,
    cotangent,
):
    rows = lax.all_gather(residual_in, "head", axis=1, tiled=True)
    batches, local_len = (rows.shape[0], rows.shape[1])
    inner_here = gate_weight.shape[0]
    heads_here = step_weight.shape[0]
    tokens = batches * local_len
    row_scale = lax.rsqrt(jnp.mean(rows * rows, axis=2, keepdims=True) + EPSILON)
    normed = (rows * row_scale * norm_gain).reshape(tokens, D)
    joined_weight = jnp.concatenate([gate_weight, inner_weight, bc_weight.T, step_weight], 0)
    projected = product_rows(normed, joined_weight)
    conv_end = 2 * inner_here + 2 * NSTATE
    gate_pre = projected[:, :inner_here]
    conv_pre = projected[:, inner_here:conv_end].reshape(
        batches, local_len, inner_here + 2 * NSTATE
    )
    step_arg = projected[:, conv_end:].reshape(batches, local_len, heads_here) + step_bias
    kernel = jnp.concatenate([conv_inner_weight, conv_bc_weight], 1)
    kernel_bias = jnp.concatenate([conv_inner_bias, conv_bc_bias], 0)
    edges = shifted(conv_pre[:, local_len - (WIDTH - 1) :], "seq", 1)
    padded = jnp.concatenate([edges, conv_pre], 1)
    conv_out = jnp.zeros_like(conv_pre) + kernel_bias
    for offset in range(WIDTH):
        conv_out = conv_out + kernel[offset] * padded[:, offset : offset + local_len]
    activated = jax.nn.silu(conv_out)
    inner_x = activated[..., :inner_here].reshape(batches, local_len, heads_here, HEADDIM)
    write_rows = activated[..., inner_here : inner_here + NSTATE]
    read_rows = activated[..., inner_here + NSTATE :]
    step_size = jax.nn.softplus(step_arg)
    rate_vec = -jnp.exp(decay_log)
    (cumulative, states), pull_blocks = jax.vjp(
        block_parts, inner_x, step_size, rate_vec, write_rows
    )
    (device_state, device_log, entering, prefix), pull_summary = jax.vjp(
        device_summary, cumulative, states
    )
    device_decay = jnp.exp(device_log)
    state_in = entering_2(
        (device_decay, device_state),
        "seq",
        link_states,
        (jnp.ones_like(device_decay), jnp.zeros_like(device_state)),
        False,
    )[1]
    ssd_out, pull_output = jax.vjp(
        block_output,
        cumulative,
        entering,
        prefix,
        inner_x,
        step_size,
        write_rows,
        read_rows,
        state_in,
    )
    mixed = ssd_out + skip_gain[:, None] * inner_x
    mixed_flat = mixed.reshape(batches, local_len, inner_here)
    gate_act = jax.nn.silu(gate_pre).reshape(batches, local_len, inner_here)
    gated = mixed_flat * gate_act
    squares = lax.psum(jnp.sum(gated * gated, axis=2), "head")
    gate_scale = lax.rsqrt(squares / DI + EPSILON)[..., None]
    normed_gate = (gated * gate_scale * gated_gain).reshape(tokens, inner_here)
    partial_out = product(normed_gate, out_weight).reshape(batches, local_len, D)
    result = residual_in + lax.psum_scatter(partial_out, "head", scatter_dimension=1, tiled=True)
    grad_rows = lax.all_gather(cotangent, "head", axis=1, tiled=True).reshape(tokens, D)
    out_weight_grad = product_cols(normed_gate, grad_rows)
    grad_normed_gate = product_rows(grad_rows, out_weight).reshape(batches, local_len, inner_here)
    gated_gain_grad = jnp.sum(grad_normed_gate * gated * gate_scale, axis=(0, 1))
    grad_scaled = grad_normed_gate * gated_gain
    cross = lax.psum(jnp.sum(grad_scaled * gated, axis=2), "head")
    grad_gated = gate_scale * grad_scaled - gated * gate_scale**3 * (cross[..., None] / DI)
    grad_mixed = (grad_gated * gate_act).reshape(batches, local_len, heads_here, HEADDIM)
    grad_gate_pre = (grad_gated * mixed_flat).reshape(tokens, inner_here) * swish_slope(gate_pre)
    skip_gain_grad = jnp.sum(grad_mixed * inner_x, axis=(0, 1, 3))
    (
        grad_cum_out,
        grad_entering,
        grad_prefix,
        grad_inner_out,
        grad_step_out,
        grad_write_out,
        grad_read,
        grad_state_in,
    ) = pull_output(grad_mixed)
    grad_state_out = entering_2(
        (device_decay, grad_state_in),
        "seq",
        link_states,
        (jnp.ones_like(device_decay), jnp.zeros_like(grad_state_in)),
        True,
    )[1]
    grad_device_log = device_decay * jnp.sum(grad_state_out * state_in, axis=(2, 3))
    grad_cum_sum, grad_states = pull_summary(
        (grad_state_out, grad_device_log, grad_entering, grad_prefix)
    )
    grad_inner_part, grad_step_part, rate_grad, grad_write_part = pull_blocks(
        (grad_cum_out + grad_cum_sum, grad_states)
    )
    grad_inner = grad_inner_out + grad_inner_part + skip_gain[:, None] * grad_mixed
    grad_step = grad_step_out + grad_step_part
    decay_log_grad = rate_grad * rate_vec
    grad_step_arg = grad_step * jax.nn.sigmoid(step_arg)
    step_bias_grad = jnp.sum(grad_step_arg, axis=(0, 1))
    grad_act = jnp.concatenate(
        [
            grad_inner.reshape(batches, local_len, inner_here),
            grad_write_out + grad_write_part,
            grad_read,
        ],
        2,
    )
    grad_conv = grad_act * swish_slope(conv_out)
    conv_bias_grad = jnp.sum(grad_conv, axis=(0, 1))
    kernel_grad = jnp.stack(
        [
            jnp.sum(grad_conv * padded[:, offset : offset + local_len], axis=(0, 1))
            for offset in range(WIDTH)
        ],
        0,
    )
    grad_padded = jnp.zeros_like(padded)
    for offset in range(WIDTH):
        grad_padded = grad_padded + jnp.pad(
            kernel[offset] * grad_conv, ((0, 0), (offset, WIDTH - 1 - offset), (0, 0))
        )
    back_edges = shifted(grad_padded[:, : WIDTH - 1], "seq", -1)
    grad_conv_pre = grad_padded[:, WIDTH - 1 :] + jnp.pad(
        back_edges, ((0, 0), (local_len - (WIDTH - 1), 0), (0, 0))
    )
    grad_projected = jnp.concatenate(
        [
            grad_gate_pre,
            grad_conv_pre.reshape(tokens, inner_here + 2 * NSTATE),
            grad_step_arg.reshape(tokens, heads_here),
        ],
        1,
    )
    joined_grad = product_cols(grad_projected, normed)
    grad_normed_part = product(grad_projected, joined_weight).reshape(batches, local_len, D)
    gate_weight_grad = joined_grad[:inner_here]
    inner_weight_grad = joined_grad[inner_here : 2 * inner_here]
    bc_part = joined_grad[2 * inner_here : conv_end].T
    step_weight_grad = joined_grad[conv_end:]
    conv_inner_weight_grad = kernel_grad[:, :inner_here]
    conv_bc_part = kernel_grad[:, inner_here:]
    conv_inner_bias_grad = conv_bias_grad[:inner_here]
    conv_bias_part = conv_bias_grad[inner_here:]
    own_scale = lax.rsqrt(jnp.mean(residual_in * residual_in, axis=2, keepdims=True) + EPSILON)
    grad_normed = lax.psum_scatter(grad_normed_part, "head", scatter_dimension=1, tiled=True)
    gain_part = jnp.sum(grad_normed * residual_in * own_scale, axis=(0, 1))
    norm_gain_grad, bc_weight_grad, conv_bc_weight_grad, conv_bc_bias_grad = lax.psum(
        (gain_part, bc_part, conv_bc_part, conv_bias_part), "head"
    )
    grad_hat = grad_normed * norm_gain
    row_cross = jnp.sum(grad_hat * residual_in, axis=2)
    residual_grad = (
        cotangent + own_scale * grad_hat - residual_in * own_scale**3 * (row_cross[..., None] / D)
    )
    totals = lax.psum(
        (
            norm_gain_grad,
            gate_weight_grad,
            inner_weight_grad,
            bc_weight_grad,
            step_weight_grad,
            conv_inner_weight_grad,
            conv_inner_bias_grad,
            conv_bc_weight_grad,
            conv_bc_bias_grad,
            step_bias_grad,
            decay_log_grad,
            skip_gain_grad,
            gated_gain_grad,
            out_weight_grad,
        ),
        "seq",
    )
    return (result, residual_grad) + tuple(totals)


def solution(mesh):
    placed = (
        P(None, ("seq", "head"), None),
        P(),
        P("head", None),
        P("head", None),
        P(),
        P("head", None),
        P(None, "head"),
        P("head"),
        P(),
        P(),
        P("head"),
        P("head"),
        P("head"),
        P("head"),
        P("head", None),
        P(None, ("seq", "head"), None),
    )
    return jax.shard_map(
        on_device,
        mesh=mesh,
        in_specs=placed,
        out_specs=(
            P(None, ("seq", "head"), None),
            P(None, ("seq", "head"), None),
            P(),
            P("head", None),
            P("head", None),
            P(),
            P("head", None),
            P(None, "head"),
            P("head"),
            P(),
            P(),
            P("head"),
            P("head"),
            P("head"),
            P("head"),
            P("head", None),
        ),
        check_vma=False,
    )
```

profile of v0, /device:TPU:0, one launch (start us, length us, event | category | flops | bytes accessed | tf_op | source)
XLA Modules:
  0.0 911.9 jit_solution(1972719444603095749)
XLA Ops:
  10.2 3.0 copy.117
  15.9 95.8 %all-gather.5.cloned.1.call-done = f32[1,1024,1536]{2,1,0:T(8,128)} async-done(((f32[1,128,1536]{2,1,0:T(8,128)}), f32[1,1024,1536]{2,1,0:T(8,128)}) %all-gather.5.cloned.1.call-update) | async-done | bytes 6291472 | tf_op jit(solution)/shard_map/all_gather | solution.py:137
  111.7 3.4 multiply_reduce_fusion.2
  116.3 26.7 %fusion.8 = f32[1024,1030]{0,1:T(8,128)S(1)} fusion(f32[1,1024,1536]{2,1,0:T(8,128)S(1)} %copy-done.21, f32[6,1536]{1,0:T(8,128)S(1)} %copy-done.97, f32[256,1536]{1,0:T(8,128)} %copy.117, f32[384,1536]{1,0:T(8,128)} %param.23, f32[384,1536]{1,0:T(8,128)} %param.22, f32[1536]{0:T(1024)S(1)} %copy-done.62, f32[1024]{0:T(1024)S(1)} %add_rsqrt_fusion.1), kind=kOutput, calls=%fused_computation.13 | convolution fusion | flops 19448492032 | bytes 16848896 | tf_op jit(solution)/shard_map/dot_general | solution.py:45
  148.3 7.1 all-reduce.15
  156.1 8.4 fusion.38
  177.5 2.9 reshape.802
  180.3 3.2 fusion.62
  187.3 9.7 %all_gather.21 = f32[4,1,6,64,128]{4,3,2,1,0:T(8,128)} all-gather(f32[1,1,6,64,128]{4,3,2,1,0:T(8,128)S(1)} %get-tuple-element.459), channel_id=1, replica_groups=mesh['seq'=4,'head'=8] {'seq'}, dimensions={0}, use_global_device_ids=true | all-gather | bytes 983040 | tf_op jit(solution)/shard_map/all_gather | solution.py:26
  197.0 6.8 while.30
  203.9 2.8 fusion.90
  206.8 7.4 fusion.40
  216.0 4.0 multiply_reduce_fusion.10
  219.9 19.3 %psum.140 = f32[1,1024]{1,0:T(1,128)} all-reduce(f32[1,1024]{1,0:T(1,128)} %bitcast.390), channel_id=1, replica_groups=mesh['seq'=4,'head'=8] {'head'}, use_global_device_ids=true, to_apply=%region_6.7 | all-reduce | flops 1024 | bytes 8192 | tf_op jit(solution)/shard_map/psum | solution.py:194
  240.5 11.8 %multiply_reduce_fusion.8 = (f32[384]{0:T(512)}, f32[1024]{0:T(1024)}, f32[1024,384]{0,1:T(8,128)}) fusion(f32[1024,384]{0,1:T(8,128)} %get-tuple-element.458, f32[1024]{0:T(1024)S(1)} %bitcast.374, f32[384]{0:T(512)S(1)} %copy-done.48, f32[384,1536]{1,0:T(8,128)S(1)} %copy-done, f32[1,1024,1536]{2,1,0:T(8,128)} %all-gather.7.cloned.1.call-done), kind=kOutput, calls=%fused_computation.84 | convolution fusion | flops 7250115072 | bytes 11807744 | tf_op jit(solution)/shard_map/dot_general | solution.py:45
  252.3 18.6 %psum.141 = f32[1,1024]{1,0:T(1,128)} all-reduce(f32[1,1024]{1,0:T(1,128)} %bitcast.389), channel_id=1, replica_groups=mesh['seq'=4,'head'=8] {'head'}, use_global_device_ids=true, to_apply=%region_10.11 | all-reduce | flops 1024 | bytes 8192 | tf_op jit(solution)/shard_map/psum | solution.py:204
  271.5 5.3 fusion.41
  276.8 2.9 reshape_reshape.2
  279.7 3.0 fusion.39
  282.8 3.6 fusion.72
  286.4 2.5 multiply_reduce_fusion.13
  289.0 11.0 %fusion.18 = (f32[4,6,256]{2,1,0:T(8,128)}, f32[4,6,256]{2,1,0:T(8,128)}, f32[4,6,256]{2,1,0:T(8,128)}, f32[4,256,256]{2,1,0:T(8,128)}) fusion(f32[4,6,256]{2,1,0:T(8,128)S(1)} %bitcast.369, f32[4,256,256]{2,1,0:T(8,128)S(1)} %copy-done.37, f32[4,6,256]{2,1,0:T(8,128)S(1)} %copy-done.47, pred[256,256]{1,0:T(8,128)(4,1)S(1)} %copy-done.51, ...), kind=kOutput, calls=%fused_computation.32 | convolution fusion | flops 1231271936 | bytes 5431296 | tf_op jit(solution)/shard_map/transpose(jvp(bchts,bcshp->bcthp))/dot_general | solution.py:111
  300.0 7.0 fusion.53
  307.1 8.3 all-gather.1
  315.4 6.8 while.31
  327.4 3.1 broadcast_multiply_fusion.4
  331.3 2.7 fusion.157
  338.4 2.6 copy.129
  342.4 2.6 copy.134
  347.8 4.5 multiply_multiply_fusion.3
  352.4 4.5 fusion.147
  358.0 3.9 pad_add_fusion
  362.2 3.1 multiply_reduce_fusion.7
  369.2 2.7 fusion.37
  371.9 24.6 %fusion.6 = f32[1030,1536]{1,0:T(8,128)S(1)} fusion(f32[1,1024,1536]{2,1,0:T(8,128)} %all-gather.5.cloned.1.call-done, f32[1536]{0:T(1024)S(1)} %copy-done.63, f32[1024]{0:T(1024)S(1)} %copy-done.85, f32[1024,6]{0,1:T(8,128)S(1)} %get-tuple-element.453, f32[1024,640]{0,1:T(8,128)S(1)} %fusion.37, f32[1024,384]{0,1:T(8,128)S(1)} %copy-done.33), kind=kOutput, calls=%fused_computation.11 | convolution fusion | flops 19445854208 | bytes 16848896 | tf_op jit(solution)/shard_map/dot_general | solution.py:55
  396.4 2.7 copy-done.19
  400.5 11.9 %fusion.2 = f32[384,1536]{1,0:T(8,128)} fusion(f32[1,1024,1536]{2,1,0:T(8,128)} %all-gather.7.cloned.1.call-done, f32[1024,384]{0,1:T(8,128)} %get-tuple-element.458, f32[384]{0:T(512)S(1)} %copy-done.48, f32[1024]{0:T(1024)S(1)} %bitcast.377), kind=kOutput, calls=%fused_computation.7 | convolution fusion | flops 7248543744 | bytes 10229248 | tf_op jit(solution)/shard_map/dot_general | solution.py:55
  412.4 2.5 fusion.153
  414.9 77.0 %all-reduce.22.cloned.1.call-done = f32[1536,256]{0,1:T(8,128)} async-done(((f32[1536,256]{0,1:T(8,128)}), f32[1536,256]{0,1:T(8,128)}) %all-reduce.22.cloned.1.call-update) | async-done | bytes 1572880 | tf_op jit(solution)/shard_map/psum | solution.py:285
  492.7 29.6 %convolution_bitcast_fusion = f32[1,1024,1536]{2,1,0:T(8,128)} fusion(f32[6,1536]{1,0:T(8,128)S(1)} %copy-done.98, f32[256,1536]{1,0:T(8,128)} %copy.117, f32[384,1536]{1,0:T(8,128)} %param.23, f32[384,1536]{1,0:T(8,128)} %param.22, f32[1024,6]{0,1:T(8,128)S(1)} %get-tuple-element.453, f32[1024,640]{0,1:T(8,128)} %copy-done.28, ...), kind=kOutput, calls=%fused_computation.26 | convolution fusion | flops 19447455744 | bytes 16838656 | tf_op jit(solution)/shard_map/dot_general | solution.py:41
  522.4 13.5 %convolution_bitcast_fusion.1 = f32[1,1024,1536]{2,1,0:T(8,128)} fusion(f32[384,1536]{1,0:T(8,128)S(1)} %copy-done, f32[1024,384]{0,1:T(8,128)} %get-tuple-element.458, f32[384]{0:T(512)S(1)} %copy-done.48, f32[1024]{0:T(1024)S(1)} %bitcast.378), kind=kOutput, calls=%fused_computation.27 | convolution fusion | flops 7248543744 | bytes 10229248 | tf_op jit(solution)/shard_map/dot_general | solution.py:41
  537.6 114.6 %all-reduce.24.cloned.1.call-done = (f32[384,1536]{1,0:T(8,128)}, f32[384,1536]{1,0:T(8,128)}, f32[1536,256]{0,1:T(8,128)}, f32[384,1536]{1,0:T(8,128)}) async-done(((f32[384,1536]{1,0:T(8,128)}, f32[384,1536]{1,0:T(8,128)}, f32[1536,256]{0,1:T(8,128)}, f32[384,1536]{1,0:T(8,128)}), (f32[384,1536]{1,0:T(8,128)}, f32[384,1536]{1,0:T(8,128)}, f32[1536,256]{0,1:T(8,128)}, ...) | async-done | bytes 8650768 | tf_op jit(solution)/shard_map/psum | solution.py:293
  652.1 3.0 copy.145
  655.2 118.6 %reduce-scatter.5.cloned.1.call-done = f32[1,128,1536]{2,1,0:T(8,128)} async-done(((f32[1,1024,1536]{2,1,0:T(8,128)}), f32[1,128,1536]{2,1,0:T(8,128)}) %reduce-scatter.5.cloned.1.call-update) | async-done | bytes 786448 | tf_op jit(solution)/shard_map/reduce_scatter | solution.py:283
  775.1 37.1 %all-reduce.16 = (f32[1536]{0:T(1024)S(1)}, f32[4,256]{1,0:T(4,128)S(1)}, f32[256]{0:T(256)S(1)}) all-reduce(f32[1536]{0:T(1024)S(1)} %get-tuple-element.398, f32[4,256]{1,0:T(4,128)S(1)} %pad_maximum_fusion.8, f32[256]{0:T(256)S(1)} %slice.139), channel_id=1, replica_groups=mesh['seq'=4,'head'=8] {'head'}, use_global_device_ids=true, to_apply=%region_30.31 | all-reduce | flops 2816 | bytes 22528 | tf_op jit(solution)/shard_map/psum | solution.py:285
  812.2 12.3 %all-reduce.17 = (f32[1536]{0:T(1024)}, f32[6,1536]{1,0:T(8,128)}, f32[4,384]{1,0:T(4,128)}, f32[384]{0:T(512)}, f32[4,256]{1,0:T(4,128)}, /*index=5*/f32[256]{0...) all-reduce(f32[1536]{0:T(1024)S(1)} %get-tuple-element.433, ...), channel_id=1, replica_groups=mesh['seq'=4,'head'=8] {'seq'}, use_global_device_ids=true, to_apply=%region_31.32 | all-reduce | flops 14354 | bytes 114832 | tf_op jit(solution)/shard_map/psum | solution.py:293
  824.5 70.5 %reduce-scatter.3.cloned.1.call-done = f32[1,128,1536]{2,1,0:T(8,128)} async-done(((f32[1,1024,1536]{2,1,0:T(8,128)}), f32[1,128,1536]{2,1,0:T(8,128)}) %reduce-scatter.3.cloned.1.call-update) | async-done | bytes 786448 | tf_op jit(solution)/shard_map/reduce_scatter | solution.py:198
  895.0 3.2 multiply_subtract_fusion.1
  (331 shorter events, 76.7 us)
Async XLA Ops:
  7.2 233.3 %copy-start = (f32[384,1536]{1,0:T(8,128)S(1)}, f32[384,1536]{1,0:T(8,128)}, u32[]{:S(2)}) copy-start(f32[384,1536]{1,0:T(8,128)} %param.34) | copy-start | bytes 7077892
  7.2 6.0 copy-start.101
  7.2 7.3 copy-start.93
  7.2 7.3 copy-start.92
  7.2 7.9 copy-start.78
  7.2 7.9 copy-start.83
  7.2 8.6 copy-start.99
  7.3 104.4 %all-gather.5.cloned.1.call-start = ((), (), s32[]{:S(2)}) async-start(), calls=%async_computation.2 | async-start | bytes 7077888 | tf_op jit(solution)/shard_map/all_gather | solution.py:137
  8.0 232.5 %all-gather.7.cloned.1.call-start = ((), (), s32[]{:S(2)}) async-start(), calls=%async_computation.4 | async-start | bytes 7077888 | tf_op jit(solution)/shard_map/all_gather | solution.py:199
  8.7 483.2 %all-reduce.22.cloned.1.call-start = ((), (), s32[]{:S(2)}) async-start(), calls=%async_computation.6 | async-start | bytes 3145728 | tf_op jit(solution)/shard_map/psum | solution.py:285
  15.1 100.0 %copy-start.97 = (f32[6,1536]{1,0:T(8,128)S(1)}, f32[6,1536]{1,0:T(8,128)}, u32[]{:S(2)}) copy-start(f32[6,1536]{1,0:T(8,128)} %param.25) | copy-start | bytes 110596
  15.8 140.3 %copy-start.52 = (f32[640]{0:T(1024)}, f32[640]{0:T(1024)S(1)}, u32[]{:S(2)}) copy-start(f32[640]{0:T(1024)S(1)} %get-tuple-element.410) | copy-start | bytes 7684
  15.8 140.3 %copy-start.54 = (f32[640]{0:T(1024)}, f32[640]{0:T(1024)S(1)}, u32[]{:S(2)}) copy-start(f32[640]{0:T(1024)S(1)} %get-tuple-element.411) | copy-start | bytes 7684
  15.8 140.3 %copy-start.56 = (f32[640]{0:T(1024)}, f32[640]{0:T(1024)S(1)}, u32[]{:S(2)}) copy-start(f32[640]{0:T(1024)S(1)} %get-tuple-element.412) | copy-start | bytes 7684
  15.9 128.8 %copy-start.88 = (f32[6]{0:T(128)}, f32[6]{0:T(128)S(1)}, u32[]{:S(2)}) copy-start(f32[6]{0:T(128)S(1)} %exponential_negate_fusion) | copy-start | bytes 76
  15.9 99.3 %copy-start.62 = (f32[1536]{0:T(1024)S(1)}, f32[1536]{0:T(1024)}, u32[]{:S(2)}) copy-start(f32[1536]{0:T(1024)} %param.21) | copy-start | bytes 18436
  116.3 26.7 %copy-start.84 = (f32[1024]{0:T(1024)}, f32[1024]{0:T(1024)S(1)}, u32[]{:S(2)}) copy-start(f32[1024]{0:T(1024)S(1)} %add_rsqrt_fusion.1) | copy-start | bytes 12292
  143.4 12.7 %collective-permute-start = (f32[1,3,640]{1,2,0:T(8,128)S(1)}, f32[1,3,640]{1,2,0:T(8,128)S(1)}, u32[]{:S(2)}, u32[]{:S(2)}) collective-permute-start(f32[1,3,640]{1,2,0:T(8,128)S(1)} %slice.142), channel_id=1, source_target_pairs={{0,8},{8,16},{16,24},{1,9},{9,17},{17,25},{2,10},{10,18},{18,26},{... | collective-permute-start | bytes 23048 | tf_op jit(solution)/shard_map/ppermute | solution.py:21
  145.7 154.3 %copy-start.43 = (f32[1024,6]{0,1:T(8,128)}, f32[1024,6]{0,1:T(8,128)S(1)}, u32[]{:S(2)}) copy-start(f32[1024,6]{0,1:T(8,128)S(1)} %get-tuple-element.462) | copy-start | bytes 73732
  146.1 18.5 %copy-start.45 = (f32[4,6,256]{2,1,0:T(8,128)}, f32[4,6,256]{2,1,0:T(8,128)S(1)}, u32[]{:S(2)}) copy-start(f32[4,6,256]{2,1,0:T(8,128)S(1)} %fusion.97) | copy-start | bytes 73732
  146.3 18.2 %copy-start.95 = (f32[6]{0:T(128)}, f32[6]{0:T(128)S(1)}, u32[]{:S(2)}) copy-start(f32[6]{0:T(128)S(1)} %get-tuple-element.407) | copy-start | bytes 76
  146.3 18.2 %copy-start.68 = (f32[1,4,6]{2,1,0:T(4,128)}, f32[1,4,6]{2,1,0:T(4,128)S(1)}, u32[]{:S(2)}) copy-start(f32[1,4,6]{2,1,0:T(4,128)S(1)} %reduce_window_sum.24) | copy-start | bytes 292
  156.1 8.5 copy-start.34
  177.5 6.1 copy-start.73
  177.5 6.1 copy-start.75
  187.3 16.6 %copy-start.70 = (f32[4,6]{1,0:T(4,128)S(1)}, f32[4,6]{1,0:T(4,128)}, u32[]{:S(2)}) copy-start(f32[4,6]{1,0:T(4,128)} %fusion.126) | copy-start | bytes 292
  206.8 7.5 copy-start.22
  216.0 24.5 %copy-start.48 = (f32[384]{0:T(512)S(1)}, f32[384]{0:T(512)}, u32[]{:S(2)}) copy-start(f32[384]{0:T(512)} %param.33) | copy-start | bytes 4612
  271.5 5.3 copy-start.59
  307.1 15.1 %copy-start.74 = (f32[6]{0:T(128)S(1)}, f32[6]{0:T(128)}, u32[]{:S(2)}) copy-start(f32[6]{0:T(128)} %get-tuple-element.487) | copy-start | bytes 76
  307.1 15.2 %copy-start.76 = (f32[6]{0:T(128)S(1)}, f32[6]{0:T(128)}, u32[]{:S(2)}) copy-start(f32[6]{0:T(128)} %get-tuple-element.489) | copy-start | bytes 76
  307.1 15.2 %copy-start.80 = (f32[6]{0:T(128)S(1)}, f32[6]{0:T(128)}, u32[]{:S(2)}) copy-start(f32[6]{0:T(128)} %get-tuple-element.488) | copy-start | bytes 76
  307.1 15.2 %copy-start.82 = (f32[6]{0:T(128)S(1)}, f32[6]{0:T(128)}, u32[]{:S(2)}) copy-start(f32[6]{0:T(128)} %get-tuple-element.490) | copy-start | bytes 76
  327.4 19.3 %slice-start = ((s8[4227072]{0:T(1024)(128)(4,1)}), s8[32768]{0:T(1024)(128)(4,1)S(1)}, s32[]{:S(2)}) async-start(s8[4227072]{0:T(1024)(128)(4,1)} %bitcast.338), calls=%async_computation.8 | async-start | bytes 65536
  338.4 8.3 slice-start.1
  340.9 5.7 copy-start.15
  341.0 5.7 copy-start.60
  362.0 5.3 copy-start.64
  362.0 5.3 copy-start.87
  362.0 5.3 copy-start.89
  365.6 3.5 collective-permute-start.1
  371.8 24.6 %copy-start.28 = (f32[1024,640]{0,1:T(8,128)}, f32[1024,640]{0,1:T(8,128)S(1)}, u32[]{:S(2)}) copy-start(f32[1024,640]{0,1:T(8,128)S(1)} %fusion.37) | copy-start | bytes 7864324
  400.4 251.7 %all-reduce.24.cloned.1.call-start = ((), (), s32[]{:S(2)}) async-start(), calls=%async_computation.7 | async-start | bytes 17301504 | tf_op jit(solution)/shard_map/psum | solution.py:293
  400.4 11.9 %copy-start.20 = (f32[1030,1536]{1,0:T(8,128)S(1)}, f32[1030,1536]{1,0:T(8,128)}, u32[]{:S(2)}) copy-start(f32[1030,1536]{1,0:T(8,128)} %copy-done.19) | copy-start | bytes 18984964
  492.0 281.8 %reduce-scatter.5.cloned.1.call-start = ((), (), s32[]{:S(2)}) async-start(), calls=%async_computation.5 | async-start | bytes 7077888 | tf_op jit(solution)/shard_map/reduce_scatter | solution.py:283
  522.3 372.7 %reduce-scatter.3.cloned.1.call-start = ((), (), s32[]{:S(2)}) async-start(), calls=%async_computation.3 | async-start | bytes 7077888 | tf_op jit(solution)/shard_map/reduce_scatter | solution.py:198
  537.2 275.0 %slice-start.2 = ((f32[1030,1536]{1,0:T(8,128)}), f32[6,1536]{1,0:T(8,128)S(1)}, s32[]{:S(2)}) async-start(f32[1030,1536]{1,0:T(8,128)} %copy-done.19), calls=%async_computation.10 | async-start | bytes 98304 | tf_op jit(solution)/shard_map/slice | solution.py:277
  537.2 275.0 %copy-start.72 = (f32[384]{0:T(512)S(1)}, f32[384]{0:T(512)}, u32[]{:S(2)}) copy-start(f32[384]{0:T(512)} %get-tuple-element.391) | copy-start | bytes 4612
  (67 other events, 218.6 us)
Sparse Core Ops, SparseCore 0:
  10.3 101.4 all-gather.4
  113.9 96.8 all-gather.6
  400.5 91.3 all-reduce.21
  495.7 156.3 all-reduce.23
  655.6 118.1 reduce-scatter.4
  777.2 117.7 reduce-scatter.2
where the time goes:
time: 921 us; the launch traced here: 912 us
  waiting for transfers between devices  479 us (52%)
  matrix products  168 us (18%)
  blocking collectives  112 us (12%)
  other arithmetic  67.9 us (7%)
  local copies, waits for them, and re-layouts  65.5 us (7%)
  between operations  16.6 us (2%)
    reduce_scatter x1, waiting for transfers between devices, on_device(): lax.psum_scatter(grad_normed_part, 'head', scatter_dimension=1, tiled=True)  119 us
    psum x1, waiting for transfers between devices, on_device(): lax.psum((norm_gain_grad, gate_weight_grad, inner_weight_grad, bc_weight_...  115 us
    all_gather x1, waiting for transfers between devices, on_device(): rows = lax.all_gather(residual_in, 'head', axis=1, tiled=True)  95.8 us
    psum x1, waiting for transfers between devices, on_device(): lax.psum((gain_part, bc_part, conv_bc_part, conv_bias_part), 'head')  77 us
    reduce_scatter x1, waiting for transfers between devices, on_device(): lax.psum_scatter(partial_out, 'head', scatter_dimension=1, tiled=True)  70.5 us
    dot_general x2, matrix products, product(): jnp.dot(left_side, right_side, precision=HIGH, preferred_element_type=jnp...  43.1 us
    dot_general x2, matrix products, product_rows(): lax.dot_general(left_side, right_side, (((1,), (1,)), ((), ())), precisio...  38.4 us
    psum x1, blocking collectives, on_device(): lax.psum((gain_part, bc_part, conv_bc_part, conv_bias_part), 'head')  37.1 us
  transfers between devices with their start and end apart: 8, of which 6 were waited for; matrix products, arithmetic and copies ran while one was open for 17% of the time, Pallas kernels for 0%

commit v1 on v0

v1 whole, which is shorter than its diff:
```python
import functools

import jax
import jax.numpy as jnp
from jax import lax
from jax.experimental import pallas as pl
from jax.experimental.pallas import tpu as pltpu
from jax.sharding import PartitionSpec as P

HEADDIM = 64
NSTATE = 128
WIDTH = 4
BLOCK = 256
EPSILON = 1e-05
EXACT = lax.Precision.HIGHEST
MESH = pl.DeviceIdType.MESH
F32 = jnp.float32
BF16 = jnp.bfloat16
VMEM_LIMIT = 66000000


def dot3(left, right, left_dim, right_dim):
    dims = (((left_dim,), (right_dim,)), ((), ()))
    one = functools.partial(lax.dot_general, dimension_numbers=dims, preferred_element_type=F32)
    return one(left[0], right[0]) + (one(left[0], right[1]) + one(left[1], right[0]))


def remote(source, target, send_sem, recv_sem, seq, head):
    return pltpu.make_async_remote_copy(
        src_ref=source,
        dst_ref=target,
        send_sem=send_sem,
        recv_sem=recv_sem,
        device_id=(seq, head),
        device_id_type=MESH,
    )


def greet(seq, head, seqs, heads):
    barrier = pltpu.get_barrier_semaphore()
    for j in range(1, seqs):
        pl.semaphore_signal(
            barrier, inc=1, device_id=(lax.rem(seq + j, seqs), head), device_id_type=MESH
        )
    for j in range(1, heads):
        pl.semaphore_signal(
            barrier, inc=1, device_id=(seq, lax.rem(head + j, heads)), device_id_type=MESH
        )
    pl.semaphore_wait(barrier, seqs + heads - 2)


def inner_count(heads):
    return 2 if heads <= 8 else 4


def tail_kernel(dims, *refs):
    seqs, heads, chunk, chans, pad = dims
    (
        gp_hi, gp_lo, hat_hi, hat_lo, w_hi, w_lo, small_in, resid, cot, gain,
        resid_grad, gate_out, inner_out, bc_out, small_out,
        gph, gpl, hth, htl, wh, wl, grads, y_in, z_in, joined, keep, core_in, x_in,
        bc_part, bc_seq, bc_head, bc_full, small_all, small_head,
        load_sem, y_send, y_recv, z_send, z_recv, c_send, c_recv, x_send, x_recv,
        f_send, f_recv, o_sem, ba_s, ba_r, bb_s, bb_r, bc_s, bc_r, bd_s, bd_r,
        sa_s, sa_r, sb_s, sb_r,
    ) = refs
    width = gain.shape[1]
    ins = inner_count(heads)
    outs = heads // ins
    rounds = (seqs // 2).bit_length() - 1
    half = chans // 2
    span = 2 * chans
    seq, head = lax.axis_index("seq"), lax.axis_index("head")
    at_out, at_in = head // ins, lax.rem(head, ins)
    side = lax.rem(seq, 2)
    partner = seq + 1 - 2 * side

    loads = [
        pltpu.make_async_copy(a, b, load_sem.at[n])
        for n, (a, b) in enumerate(
            ((gp_hi, gph), (w_hi, wh), (gp_lo, gpl), (w_lo, wl), (hat_hi, hth), (hat_lo, htl))
        )
    ]
    for load in loads:
        load.start()
    mine = pl.ds(pl.multiple_of(side * half, 8), half)
    theirs = pl.ds(pl.multiple_of((1 - side) * half, 8), half)
    greet(seq, head, seqs, heads)

    core = [None] * 2
    for load in loads[:4]:
        load.wait()

    upper = at_out // (outs // 2)
    mirrored = at_out + upper * (outs - 1 - 2 * at_out)

    def target(step):
        last = (step + 1) // outs
        far = outs - 1 - step
        far = far - (mirrored - far + outs) // outs
        far = far + upper * (outs - 1 - 2 * far)
        return far + last * (at_out - far)

    def chunk_grad(step, inside):
        where = target(step) * ins + inside
        rows = pl.ds(pl.multiple_of(where * chunk, 8), chunk)
        grads[where] = dot3((gph[rows, :], gpl[rows, :]), (wh[...], wl[...]), 1, 0)
        return where

    def y_copy(step, j):
        to = lax.rem(at_in + 1 + j, ins)
        where = target(step) * ins + to
        slot = target(step) * (ins - 1) + j
        return remote(
            grads.at[where],
            y_in.at[slot],
            y_send.at[slot],
            y_recv.at[slot],
            seq,
            at_out * ins + to,
        )

    @pl.loop(0, outs)
    def _(step):
        for j in range(ins - 1):
            chunk_grad(step, lax.rem(at_in + 1 + j, ins))
            y_copy(step, j).start()

    x_copies = {}

    def x_start(n, source, turn):
        far = seq + (2 << turn) - 2 * (2 << turn) * lax.rem(seq // (2 << turn), 2)
        x_copies[n, turn] = remote(
            source, x_in.at[n, turn], x_send.at[n, turn], x_recv.at[n, turn], far, head
        )
        x_copies[n, turn].start()

    def after_core(n):
        core[n].wait()
        keep[n] = keep[n] + core_in[n]
        x_start(n, keep.at[n], 0)

    finals = {}
    puts = {}

    def after_x(n, result):
        now, new = keep, core_in
        for turn in range(rounds):
            x_copies[n, turn].wait()
            new[n] = now[n] + x_in[n, turn]
            now, new = new, now
            if turn + 1 < rounds:
                x_start(n, now.at[n], turn + 1)
        puts[n] = pltpu.make_async_copy(now.at[n], result.at[mine], o_sem.at[n])
        puts[n].start()
        finals[n] = remote(
            now.at[n], result.at[mine], f_send.at[n], f_recv.at[n], partner, head
        )
        finals[n].start()

    for load in loads[4:]:
        load.wait()
    joined[span:, :] = dot3(
        (gph[:, span:], gpl[:, span:]), (hth[...], htl[...]), 0, 0
    )
    gain_row = gain[...]
    pieces, _, lanes = bc_part.shape
    across = width // lanes

    def w_rows(lo, hi):
        return wh[lo:hi, :].astype(F32) + wl[lo:hi, :].astype(F32)

    gain_part = jnp.sum(joined[span:, :] * w_rows(span, pad), axis=0, keepdims=True)
    for row in range(pieces // across):
        for col in range(across):
            lane = slice(col * lanes, (col + 1) * lanes)
            block = joined[span + row * 8 : span + row * 8 + 8, lane] * gain_row[:, lane]
            bc_part[row * across + col] = block
    ba = []
    for j in range(1, seqs):
        to = lax.rem(seq + j, seqs)
        ba.append(
            remote(
                bc_part.at[pl.ds(to * heads, heads)],
                bc_seq.at[j - 1],
                ba_s.at[j - 1],
                ba_r.at[j - 1],
                to,
                head,
            )
        )
        ba[-1].start()

    @pl.loop(0, outs)
    def _(step):
        chunk_grad(step, at_in)

    def weight_rows(n):
        lo = n * chans
        if chans % 128 == 0:
            joined[lo : lo + chans, :] = dot3(
                (gph[:, lo : lo + chans], gpl[:, lo : lo + chans]), (hth[...], htl[...]), 0, 0
            )
        elif n == 0:
            joined[:span, :] = dot3((gph[:, :span], gpl[:, :span]), (hth[...], htl[...]), 0, 0)
        part = jnp.sum(joined[lo : lo + chans, :] * w_rows(lo, lo + chans), 0, keepdims=True)
        joined[lo : lo + chans, :] = joined[lo : lo + chans, :] * gain_row
        keep[n] = joined[pl.ds(pl.multiple_of(lo + side * half, 8), half), :]
        core[n] = remote(
            joined.at[pl.ds(pl.multiple_of(lo + (1 - side) * half, 8), half)],
            core_in.at[n],
            c_send.at[n],
            c_recv.at[n],
            partner,
            head,
        )
        core[n].start()
        return part

    def z_copy(where, step, up):
        goal = target(step)
        return remote(
            grads.at[where],
            z_in.at[goal + (1 if up else 0)],
            z_send.at[step],
            z_recv.at[goal + (1 if up else 0)],
            seq,
            (at_out + (1 if up else -1)) * ins + at_in,
        )

    def z_wait(slot):
        remote(
            grads.at[0], z_in.at[slot], z_send.at[0], z_recv.at[slot], partner, head
        ).wait_recv()

    def reduce_step(step):
        goal = target(step)
        where = goal * ins + at_in
        for j in range(ins - 1):
            y_copy(step, j).wait_recv()
            grads[where] = grads[where] + y_in[goal * (ins - 1) + j]
        if step == outs - 1:

            @pl.when(at_out > 0)
            def _():
                z_wait(goal + 1)
                grads[where] = grads[where] + z_in[goal + 1]

            @pl.when(at_out < outs - 1)
            def _():
                z_wait(goal)
                grads[where] = grads[where] + z_in[goal]

            return

        @pl.when(goal > at_out)
        def _():
            @pl.when(at_out > 0)
            def _():
                z_wait(goal + 1)
                grads[where] = grads[where] + z_in[goal + 1]

            z_copy(where, step, True).start()

        @pl.when(goal < at_out)
        def _():
            @pl.when(at_out < outs - 1)
            def _():
                z_wait(goal)
                grads[where] = grads[where] + z_in[goal]

            z_copy(where, step, False).start()

    gain_part = gain_part + weight_rows(0)
    reduce_step(0)
    gain_part = gain_part + weight_rows(1)
    after_core(0)

    small_all[seq] = small_in[...]
    small_all[seq, 0] = joined[span + 2 * NSTATE : span + 2 * NSTATE + 8, :] * gain_row
    small_all[seq, 2, 0:1, :] = gain_part
    sa = []
    for j in range(1, seqs):
        sa.append(
            remote(
                small_all.at[seq],
                small_all.at[seq],
                sa_s.at[j - 1],
                sa_r.at[j - 1],
                lax.rem(seq + j, seqs),
                head,
            )
        )
        sa[-1].start()
    after_core(1)

    for copy in ba:
        copy.wait_recv()
    own = pl.ds(seq * heads, heads)
    bc_part[own] = bc_part[own] + bc_seq[0]
    for j in range(1, seqs - 1):
        bc_part[own] = bc_part[own] + bc_seq[j]
    bb = []
    for j in range(1, heads):
        to = lax.rem(head + j, heads)
        bb.append(
            remote(
                bc_part.at[seq * heads + to],
                bc_head.at[j - 1],
                bb_s.at[j - 1],
                bb_r.at[j - 1],
                seq,
                to,
            )
        )
        bb[-1].start()

    def sent_from(j, count, at):
        return lax.rem(at - j + count, count)

    for j in range(1, seqs):
        came = sent_from(j, seqs, seq)
        remote(
            small_all.at[came], small_all.at[came], sa_s.at[j - 1], sa_r.at[j - 1], partner, head
        ).wait_recv()
    total = small_all[0]
    for j in range(1, seqs):
        total = total + small_all[j]
    small_out[...] = total
    small_head[head] = total[2]
    sb = []
    for j in range(1, heads):
        sb.append(
            remote(
                small_head.at[head],
                small_head.at[head],
                sb_s.at[j - 1],
                sb_r.at[j - 1],
                seq,
                lax.rem(head + j, heads),
            )
        )
        sb[-1].start()

    reduce_step(1)
    for copy in bb:
        copy.wait_recv()
    piece = bc_part[seq * heads + head]
    for j in range(heads - 1):
        piece = piece + bc_head[j]
    here = seq * heads + head
    bc_full[here] = piece
    bc = []
    for j in range(1, heads):
        bc.append(
            remote(
                bc_full.at[here],
                bc_full.at[here],
                bc_s.at[j - 1],
                bc_r.at[j - 1],
                seq,
                lax.rem(head + j, heads),
            )
        )
        bc[-1].start()
    for j in range(1, heads):
        came = sent_from(j, heads, head)
        remote(
            small_head.at[came], small_head.at[came], sb_s.at[j - 1], sb_r.at[j - 1], seq, came
        ).wait_recv()
    total = small_head[0]
    for j in range(1, heads):
        total = total + small_head[j]
    small_out[2] = total
    for j in range(1, heads):
        came = seq * heads + sent_from(j, heads, head)
        remote(
            bc_full.at[came], bc_full.at[came], bc_s.at[j - 1], bc_r.at[j - 1], partner, head
        ).wait_recv()
    bd = []
    for j in range(1, seqs):
        bd.append(
            remote(
                bc_full.at[own],
                bc_full.at[own],
                bd_s.at[j - 1],
                bd_r.at[j - 1],
                lax.rem(seq + j, seqs),
                head,
            )
        )
        bd[-1].start()
    for step in range(2, outs - 1):
        reduce_step(step)
    after_x(0, gate_out)
    reduce_step(outs - 1)
    where = at_out * ins + at_in
    grad_hat = grads[where] * gain_row
    rows = resid[...]
    scale = lax.rsqrt(jnp.mean(rows * rows, axis=1, keepdims=True) + EPSILON)
    row_cross = jnp.sum(grad_hat * rows, axis=1, keepdims=True)
    resid_grad[...] = (
        cot[...] + scale * grad_hat - rows * (scale * scale * scale * (row_cross / width))
    )
    after_x(1, inner_out)
    for j in range(1, seqs):
        came = pl.ds(sent_from(j, seqs, seq) * heads, heads)
        remote(
            bc_full.at[came], bc_full.at[came], bd_s.at[j - 1], bd_r.at[j - 1], partner, head
        ).wait_recv()
    bc_put = pltpu.make_async_copy(bc_full, bc_out, o_sem.at[2])
    bc_put.start()

    @pl.loop(0, outs)
    def _(step):
        for j in range(ins - 1):
            y_copy(step, j).wait_send()

    for step in range(outs - 1):
        remote(
            grads.at[0], z_in.at[0], z_send.at[step], z_recv.at[0], partner, head
        ).wait_send()
    for copy in ba + bb + bc + bd + sa + sb:
        copy.wait_send()
    for n in range(2):
        finals[n].wait_send()
        remote(
            keep.at[n],
            (gate_out, inner_out)[n].at[theirs],
            f_send.at[n],
            f_recv.at[n],
            partner,
            head,
        ).wait_recv()
        puts[n].wait()
    bc_put.wait()


def tail(gp, hat, weight, small, resid, cot, gain, seqs, heads, chans):
    tokens, width = hat[0].shape
    chunk = tokens // heads
    pad = gp[0].shape[1]
    ins = inner_count(heads)
    outs = heads // ins
    rounds = (seqs // 2).bit_length() - 1
    half = chans // 2
    lanes = 2 * NSTATE * width // (8 * seqs * heads)
    pieces = seqs * heads
    anywhere = pl.BlockSpec(memory_space=pl.ANY)
    local = pl.BlockSpec(memory_space=pltpu.VMEM)
    sems = pltpu.SemaphoreType.DMA
    weight_shape = jax.ShapeDtypeStruct((chans, width), F32)
    return pl.pallas_call(
        functools.partial(tail_kernel, (seqs, heads, chunk, chans, pad)),
        out_shape=(
            jax.ShapeDtypeStruct((chunk, width), F32),
            weight_shape,
            weight_shape,
            jax.ShapeDtypeStruct((pieces, 8, lanes), F32),
            jax.ShapeDtypeStruct((3, 8, width), F32),
        ),
        in_specs=[anywhere] * 6 + [local] * 4,
        out_specs=(local, anywhere, anywhere, anywhere, local),
        scratch_shapes=[
            pltpu.VMEM((tokens, pad), BF16),
            pltpu.VMEM((tokens, pad), BF16),
            pltpu.VMEM((tokens, width), BF16),
            pltpu.VMEM((tokens, width), BF16),
            pltpu.VMEM((pad, width), BF16),
            pltpu.VMEM((pad, width), BF16),
            pltpu.VMEM((heads, chunk, width), F32),
            pltpu.VMEM((outs * (ins - 1), chunk, width), F32),
            pltpu.VMEM((outs + 1, chunk, width), F32),
            pltpu.VMEM((pad, width), F32),
            pltpu.VMEM((2, half, width), F32),
            pltpu.VMEM((2, half, width), F32),
            pltpu.VMEM((2, rounds, half, width), F32),
            pltpu.VMEM((pieces, 8, lanes), F32),
            pltpu.VMEM((seqs - 1, heads, 8, lanes), F32),
            pltpu.VMEM((heads - 1, 8, lanes), F32),
            pltpu.VMEM((pieces, 8, lanes), F32),
            pltpu.VMEM((seqs, 3, 8, width), F32),
            pltpu.VMEM((heads, 8, width), F32),
            sems((6,)),
            sems((outs * (ins - 1),)),
            sems((outs * (ins - 1),)),
            sems((outs,)),
            sems((outs + 1,)),
            sems((2,)),
            sems((2,)),
            sems((2, rounds)),
            sems((2, rounds)),
            sems((2,)),
            sems((2,)),
            sems((3,)),
            sems((seqs - 1,)),
            sems((seqs - 1,)),
            sems((heads - 1,)),
            sems((heads - 1,)),
            sems((heads - 1,)),
            sems((heads - 1,)),
            sems((seqs - 1,)),
            sems((seqs - 1,)),
            sems((seqs - 1,)),
            sems((seqs - 1,)),
            sems((heads - 1,)),
            sems((heads - 1,)),
        ],
        compiler_params=pltpu.CompilerParams(
            collective_id=1, has_side_effects=True, vmem_limit_bytes=VMEM_LIMIT
        ),
        name="tail",
    )(*gp, *hat, *weight, small, resid, cot, gain)


def head_kernel(dims, *refs):
    heads, chunk, chans, pad = dims
    (
        rows, gain, gate_w, inner_w, bc_w, step_w,
        hat_hi, hat_lo, proj_out, w_hi, w_lo,
        parts, hth, htl, proj, raw, wh, wl, wth, wtl,
        load_sem, z_send, z_recv, y_send, y_recv, put_sem,
    ) = refs
    width = gain.shape[1]
    ins = inner_count(heads)
    outs = heads // ins
    span = 2 * chans
    seq, head = lax.axis_index("seq"), lax.axis_index("head")
    at_out, at_in = head // ins, lax.rem(head, ins)

    loads = [
        pltpu.make_async_copy(gate_w, raw.at[pl.ds(0, chans)], load_sem.at[0]),
        pltpu.make_async_copy(inner_w, raw.at[pl.ds(chans, chans)], load_sem.at[1]),
    ]
    for load in loads:
        load.start()
    greet(seq, head, 1, heads)
    values = rows[...]
    parts[head] = values * lax.rsqrt(
        jnp.mean(values * values, axis=1, keepdims=True) + EPSILON
    )

    def z_copy(where, up):
        return remote(
            parts.at[where],
            parts.at[where],
            z_send.at[where // ins, up],
            z_recv.at[where // ins],
            seq,
            (at_out + 2 * up - 1) * ins + at_in,
        )

    def y_copy(where, j, to):
        return remote(
            parts.at[where],
            parts.at[where],
            y_send.at[where // ins, j],
            y_recv.at[where // ins, j],
            seq,
            at_out * ins + to,
        )

    def arrived(place, distance, first):
        where = place * ins + at_in

        @pl.when(distance > 0)
        def _():
            z_copy(where, 0).wait_recv()

        @pl.when((place >= at_out) & (at_out > 0))
        def _():
            z_copy(where, 0).start()

        @pl.when((place <= at_out) & (at_out < outs - 1))
        def _():
            z_copy(where, 1).start()

        for j in range(ins - 1):
            y_copy(where, j, lax.rem(at_in + 1 + j, ins)).start()

    arrived(at_out, 0, True)

    raw[span : span + 2 * NSTATE, :] = bc_w[...].T
    raw[span + 2 * NSTATE :, :] = step_w[...]
    for load in loads:
        load.wait()
    gain_row = gain[...]

    @pl.loop(0, pad // 128)
    def _(block):
        here = pl.ds(pl.multiple_of(block * 128, 128), 128)
        piece = raw[here, :]
        top = piece.astype(BF16)
        wh[here, :] = top
        wl[here, :] = (piece - top.astype(F32)).astype(BF16)
        turned = (piece * gain_row).T
        top = turned.astype(BF16)
        wth[:, here] = top
        wtl[:, here] = (turned - top.astype(F32)).astype(BF16)

    puts = [
        pltpu.make_async_copy(wh, w_hi, put_sem.at[0]),
        pltpu.make_async_copy(wl, w_lo, put_sem.at[1]),
    ]
    for put in puts:
        put.start()

    def chunk_rows(where):
        return pl.ds(pl.multiple_of(where * chunk, 8), chunk)

    def chunk_puts(where):
        here = chunk_rows(where)
        return [
            pltpu.make_async_copy(hth.at[where], hat_hi.at[here], put_sem.at[2 + 3 * where]),
            pltpu.make_async_copy(htl.at[where], hat_lo.at[here], put_sem.at[3 + 3 * where]),
            pltpu.make_async_copy(proj.at[where], proj_out.at[here], put_sem.at[4 + 3 * where]),
        ]

    def project(where):
        piece = parts[where]
        top = piece.astype(BF16)
        low = (piece - top.astype(F32)).astype(BF16)
        hth[where] = top
        htl[where] = low
        proj[where] = dot3((top, low), (wth[...], wtl[...]), 1, 0)
        for put in chunk_puts(where):
            put.start()

    @pl.loop(0, outs + 1)
    def _(distance):
        for side in range(2):
            place = at_out + (2 * side - 1) * distance

            @pl.when((distance > 0) & (place >= 0) & (place < outs))
            def _():
                arrived(place, distance, False)

        @pl.loop(0, 2 * ins)
        def _(n):
            side, j = n // ins, lax.rem(n, ins)
            late = (j + ins - 1) // ins
            away = distance - late
            place = at_out + (2 * side - 1) * away

            @pl.when(
                (place >= 0) & (place < outs) & (away >= 0) & (away + 1 - side > 0)
            )
            def _():
                frm = lax.rem(at_in + ins - j, ins)
                where = place * ins + frm

                @pl.when(j > 0)
                def _():
                    y_copy(where, j - 1, lax.rem(at_in + 1, ins)).wait_recv()

                project(where)

    for place in range(outs):
        where = place * ins + at_in

        @pl.when((place >= at_out) & (at_out > 0))
        def _():
            z_copy(where, 0).wait_send()

        @pl.when((place <= at_out) & (at_out < outs - 1))
        def _():
            z_copy(where, 1).wait_send()

        for j in range(ins - 1):
            y_copy(where, j, lax.rem(at_in + 1 + j, ins)).wait_send()
    for put in puts:
        put.wait()

    @pl.loop(0, heads)
    def _(where):
        for put in chunk_puts(where):
            put.wait()


def gather_project(resid, gain, gate_w, inner_w, bc_w, step_w, heads):
    chunk, width = resid.shape
    chans = gate_w.shape[0]
    pad = 2 * chans + 2 * NSTATE + 128
    ins = inner_count(heads)
    outs = heads // ins
    tokens = chunk * heads
    anywhere = pl.BlockSpec(memory_space=pl.ANY)
    local = pl.BlockSpec(memory_space=pltpu.VMEM)
    sems = pltpu.SemaphoreType.DMA
    shape = jax.ShapeDtypeStruct
    return pl.pallas_call(
        functools.partial(head_kernel, (heads, chunk, chans, pad)),
        out_shape=(
            shape((tokens, width), BF16),
            shape((tokens, width), BF16),
            shape((tokens, pad), F32),
            shape((pad, width), BF16),
            shape((pad, width), BF16),
        ),
        in_specs=[local, local, anywhere, anywhere, local, local],
        out_specs=(anywhere,) * 5,
        scratch_shapes=[
            pltpu.VMEM((heads, chunk, width), F32),
            pltpu.VMEM((heads, chunk, width), BF16),
            pltpu.VMEM((heads, chunk, width), BF16),
            pltpu.VMEM((heads, chunk, pad), F32),
            pltpu.VMEM((pad, width), F32),
            pltpu.VMEM((pad, width), BF16),
            pltpu.VMEM((pad, width), BF16),
            pltpu.VMEM((width, pad), BF16),
            pltpu.VMEM((width, pad), BF16),
            sems((2,)),
            sems((outs, 2)),
            sems((outs,)),
            sems((outs, ins - 1)),
            sems((outs, ins - 1)),
            sems((2 + 3 * heads,)),
        ],
        compiler_params=pltpu.CompilerParams(
            collective_id=2, has_side_effects=True, vmem_limit_bytes=VMEM_LIMIT
        ),
        name="gather_project",
    )(resid, gain, gate_w, inner_w, bc_w, step_w)


def dotx(left, right, left_dim, right_dim):
    return lax.dot_general(
        left,
        right,
        (((left_dim,), (right_dim,)), ((), ())),
        precision=EXACT,
        preferred_element_type=F32,
    )


def halves(values):
    top = values.astype(BF16)
    return (top, (values - top.astype(F32)).astype(BF16))


class LineGather:
    def __init__(self, parts, sems, seq, head, heads):
        self.parts, self.seq, self.heads = parts, seq, heads
        self.z_send, self.z_recv, self.y_send, self.y_recv = sems
        self.ins = inner_count(heads)
        self.outs = heads // self.ins
        self.at_out, self.at_in = head // self.ins, lax.rem(head, self.ins)

    def z_copy(self, where, up):
        place = where // self.ins
        return remote(
            self.parts.at[where],
            self.parts.at[where],
            self.z_send.at[place, up],
            self.z_recv.at[place],
            self.seq,
            (self.at_out + 2 * up - 1) * self.ins + self.at_in,
        )

    def y_copy(self, where, j, to):
        place = where // self.ins
        return remote(
            self.parts.at[where],
            self.parts.at[where],
            self.y_send.at[place, j],
            self.y_recv.at[place, j],
            self.seq,
            self.at_out * self.ins + to,
        )

    def arrived(self, place, wait):
        where = place * self.ins + self.at_in
        if wait:
            self.z_copy(where, 0).wait_recv()

        @pl.when((place >= self.at_out) & (self.at_out > 0))
        def _():
            self.z_copy(where, 0).start()

        @pl.when((place <= self.at_out) & (self.at_out < self.outs - 1))
        def _():
            self.z_copy(where, 1).start()

        for j in range(self.ins - 1):
            self.y_copy(where, j, lax.rem(self.at_in + 1 + j, self.ins)).start()

    def start(self):
        self.arrived(self.at_out, False)

    def relay(self, distance):
        for side in range(2):
            place = self.at_out + (2 * side - 1) * distance

            @pl.when((place >= 0) & (place < self.outs))
            def _():
                self.arrived(place, True)

    def use(self, distance, consume):
        @pl.loop(0, 2 * self.ins)
        def _(n):
            side, j = n // self.ins, lax.rem(n, self.ins)
            late = (j + self.ins - 1) // self.ins
            away = distance - late
            place = self.at_out + (2 * side - 1) * away

            @pl.when(
                (place >= 0) & (place < self.outs) & (away >= 0) & (away + 1 - side > 0)
            )
            def _():
                where = place * self.ins + lax.rem(self.at_in + self.ins - j, self.ins)

                @pl.when(j > 0)
                def _():
                    self.y_copy(where, j - 1, lax.rem(self.at_in + 1, self.ins)).wait_recv()

                consume(where)

    def finish(self):
        for place in range(self.outs):
            where = place * self.ins + self.at_in

            @pl.when((place >= self.at_out) & (self.at_out > 0))
            def _():
                self.z_copy(where, 0).wait_send()

            @pl.when((place <= self.at_out) & (self.at_out < self.outs - 1))
            def _():
                self.z_copy(where, 1).wait_send()

            for j in range(self.ins - 1):
                self.y_copy(where, j, lax.rem(self.at_in + 1 + j, self.ins)).wait_send()


def lanes_of(chans):
    return [(lo, min(lo + 2 * HEADDIM, chans)) for lo in range(0, chans, 2 * HEADDIM)]


def row_scale(total_row, expand):
    wide = jnp.broadcast_to(jnp.exp(total_row), (128, 128)).T
    return dotx(expand, wide, 0, 0)


def logistic(values):
    return 1.0 / (1.0 + jnp.exp(-values))


def decay_of(cum, cum_turned, h, causal):
    gap = cum[:, h : h + 1] - cum_turned[h : h + 1, :]
    return jnp.where(causal, jnp.exp(jnp.where(causal, gap, 0.0)), 0.0)


def forward_kernel(dims, *refs):
    seqs, heads, chunk, chans, pad = dims
    (
        proj, cot, out_w, conv_p, head_p, chan_p, expand_in,
        cot_hi, cot_lo, conv_o, cum_o, step_o, state_o, mixed_o, cross_o, stat_o, edge_o,
        parts, hi, lo, pj, raw, owh, owl, scaled, enter, prefix, run, exch, stat_all, lows,
        z_send, z_recv, y_send, y_recv, load_sem, put_sem, e_send, e_recv,
        s_send, s_recv, t_send, t_recv,
    ) = refs
    tokens = chunk * heads
    blocks = tokens // BLOCK
    span = 2 * chans
    wide = chans + 2 * NSTATE
    here_heads = chans // HEADDIM
    seq, head = lax.axis_index("seq"), lax.axis_index("head")
    load = pltpu.make_async_copy(proj, pj.at[pl.ds(8, tokens)], load_sem.at[0])
    load.start()
    load_w = pltpu.make_async_copy(out_w, raw, load_sem.at[1])
    load_w.start()
    parts[head] = cot[...]
    greet(seq, head, seqs, heads)
    gather = LineGather(parts, (z_send, z_recv, y_send, y_recv), seq, head, heads)
    gather.start()
    edge = remote(
        proj.at[pl.ds(tokens - 8, 8)],
        pj.at[pl.ds(0, 8)],
        e_send,
        e_recv,
        lax.rem(seq + 1, seqs),
        head,
    )
    edge.start()
    load_w.wait()
    for lane, end in lanes_of(chans):
        owh[:, lane:end], owl[:, lane:end] = halves(raw[lane:end, :].T)
    expand = expand_in[...]
    load.wait()
    edge.wait()
    first = jnp.where(seq > 0, pj[0:8, :], 0.0)
    pj[0:8, :] = first
    edge_o[...] = first
    tri_r = lax.broadcasted_iota(jnp.int32, (BLOCK, BLOCK), 0)
    tri_c = lax.broadcasted_iota(jnp.int32, (BLOCK, BLOCK), 1)
    causal = tri_r >= tri_c
    lower = causal.astype(F32)
    run[...] = jnp.zeros_like(run)
    prefix[...] = jnp.zeros_like(prefix)

    @pl.loop(0, blocks)
    def _(b):
        at = pl.multiple_of(b * BLOCK, BLOCK)
        here = pl.ds(at, BLOCK)
        window = pj[pl.ds(at, BLOCK + 8), chans : span + 2 * NSTATE]
        conv = jnp.zeros((BLOCK, wide), F32) + conv_p[4:5, :]
        for k in range(WIDTH):
            conv = conv + conv_p[k : k + 1, :] * window[5 + k : 5 + k + BLOCK, :]
        conv_o[here, :] = conv
        act = conv * logistic(conv)
        arg = pj[pl.ds(at + 8, BLOCK), span + 2 * NSTATE : pad] + head_p[0:1, :]
        step = jnp.maximum(arg, 0.0) + jnp.log1p(jnp.exp(-jnp.abs(arg)))
        cum = dotx(lower, step * head_p[1:2, :], 1, 0)
        last = cum[BLOCK - 1 : BLOCK, :]
        step_o[here, :] = step
        cum_o[here, :] = cum
        fed = act[:, :chans] * dotx(step, expand, 1, 0)
        scaled[here, :] = fed
        fresh = dotx(
            fed * dotx(jnp.exp(last - cum), expand, 1, 0), act[:, chans : chans + NSTATE], 0, 0
        )
        enter[b] = run[...]
        run[...] = row_scale(last, expand) * run[...] + fresh
        prefix[pl.ds(b + 1, 1), :] = prefix[pl.ds(b, 1), :] + last

    gather.relay(1)
    exch[seq, 0:chans, :] = run[...]
    exch[seq, chans : chans + 8, :] = jnp.broadcast_to(prefix[blocks : blocks + 1, :], (8, 128))

    def state_copy(at, j, to):
        return remote(exch.at[at], exch.at[at], s_send.at[j - 1], s_recv.at[j - 1], to, head)

    for j in range(1, seqs):

        @pl.when(seq + j < seqs)
        def _():
            state_copy(seq, j, seq + j).start()

    @pl.loop(0, blocks)
    def _(b):
        at = pl.multiple_of(b * BLOCK, BLOCK)
        here = pl.ds(at, BLOCK)
        bc = conv_o[here, chans:wide]
        bc = bc * logistic(bc)
        scores = dotx(bc[:, NSTATE:], bc[:, :NSTATE], 1, 1)
        cum = cum_o[here, :]
        turned = cum.T
        for first_lane, end in lanes_of(chans):
            fed = scaled[here, first_lane:end]
            outs = [
                dotx(decay_of(cum, turned, lane // HEADDIM, causal) * scores, fed, 1, 0)
                for lane in range(first_lane, end, HEADDIM)
            ]
            out = outs[0]
            if len(outs) == 2:
                lane = lax.broadcasted_iota(jnp.int32, out.shape, 1)
                out = jnp.where(lane < HEADDIM, outs[0], outs[1])
            mixed_o[here, first_lane:end] = out

    if gather.outs > 2:
        gather.relay(2)
    run[...] = jnp.zeros_like(run)
    for earlier in range(seqs - 1):

        @pl.when(earlier < seq)
        def _():
            for j in range(1, seqs):

                @pl.when(seq - earlier == j)
                def _():
                    state_copy(earlier, j, lax.rem(seq + 1, seqs)).wait_recv()

            run[...] = (
                row_scale(exch[earlier, chans : chans + 1, :], expand) * run[...]
                + exch[earlier, 0:chans, :]
            )

    @pl.loop(0, blocks)
    def _(b):
        at = pl.multiple_of(b * BLOCK, BLOCK)
        here = pl.ds(at, BLOCK)
        state = enter[b] + row_scale(prefix[pl.ds(b, 1), :], expand) * run[...]
        state_o[b] = state
        conv = conv_o[here, :]
        act = conv * logistic(conv)
        gate = pj[pl.ds(at + 8, BLOCK), 0:chans]
        carried = dotx(act[:, chans + NSTATE :], state, 1, 1)
        mixed = (
            mixed_o[here, :]
            + carried * dotx(jnp.exp(cum_o[here, :]), expand, 1, 0)
            + chan_p[1:2, :] * act[:, :chans]
        )
        mixed_o[here, :] = mixed
        scaled[here, :] = mixed * gate * logistic(gate)

    for distance in range(3, gather.outs):
        gather.relay(distance)

    def chunk_puts(where):
        rows = pl.ds(pl.multiple_of(where * chunk, 8), chunk)
        return [
            pltpu.make_async_copy(hi.at[where], cot_hi.at[rows], put_sem.at[2 * where]),
            pltpu.make_async_copy(lo.at[where], cot_lo.at[rows], put_sem.at[2 * where + 1]),
        ]

    def consume(where):
        rows = pl.ds(pl.multiple_of(where * chunk, 8), chunk)
        top, low = halves(parts[where])
        hi[where] = top
        lo[where] = low
        cross_o[rows, :] = dot3((top, low), (owh[...], owl[...]), 1, 0)
        for put in chunk_puts(where):
            put.start()

    for distance in range(gather.outs + 1):
        gather.use(distance, consume)

    ones = jnp.ones((8, chans), F32)
    groups = tokens // 128
    for n in range(groups):
        here = slice(n * 128, n * 128 + 128)
        gated = scaled[here, :]
        lows[n : n + 1, :] = dotx(ones, gated * gated, 1, 1)[0:1, :]
        lows[groups + n : groups + n + 1, :] = dotx(
            ones, cross_o[here, :] * chan_p[0:1, :] * gated, 1, 1
        )[0:1, :]
    stat_all[head] = lows[...]
    sends = []
    for j in range(1, heads):
        sends.append(
            remote(
                stat_all.at[head],
                stat_all.at[head],
                t_send.at[j - 1],
                t_recv.at[j - 1],
                seq,
                lax.rem(head + j, heads),
            )
        )
        sends[-1].start()
    gather.finish()

    @pl.loop(0, heads)
    def _(where):
        for put in chunk_puts(where):
            put.wait()

    for j in range(1, seqs):

        @pl.when(seq + j < seqs)
        def _():
            state_copy(seq, j, seq + j).wait_send()

    for j in range(1, heads):
        came = lax.rem(head - j + heads, heads)
        remote(
            stat_all.at[came], stat_all.at[came], t_send.at[j - 1], t_recv.at[j - 1], seq, came
        ).wait_recv()
    total = stat_all[0]
    for j in range(1, heads):
        total = total + stat_all[j]
    stat_o[...] = total
    for copy in sends:
        copy.wait_send()


def forward(proj, cot, out_w, conv_p, head_p, chan_p, expand, seqs, heads):
    tokens, pad = proj.shape
    chunk, width = cot.shape
    chans = out_w.shape[0]
    ins = inner_count(heads)
    outs = heads // ins
    wide = chans + 2 * NSTATE
    blocks = tokens // BLOCK
    groups = 2 * tokens // 128
    anywhere = pl.BlockSpec(memory_space=pl.ANY)
    local = pl.BlockSpec(memory_space=pltpu.VMEM)
    sems = pltpu.SemaphoreType.DMA
    shape = jax.ShapeDtypeStruct
    return pl.pallas_call(
        functools.partial(forward_kernel, (seqs, heads, chunk, chans, pad)),
        out_shape=(
            shape((tokens, width), BF16),
            shape((tokens, width), BF16),
            shape((tokens, wide), F32),
            shape((tokens, 128), F32),
            shape((tokens, 128), F32),
            shape((blocks, chans, NSTATE), F32),
            shape((tokens, chans), F32),
            shape((tokens, chans), F32),
            shape((groups, 128), F32),
            shape((8, pad), F32),
        ),
        in_specs=[anywhere, local, anywhere, local, local, local, local],
        out_specs=(anywhere, anywhere) + (local,) * 8,
        scratch_shapes=[
            pltpu.VMEM((heads, chunk, width), F32),
            pltpu.VMEM((heads, chunk, width), BF16),
            pltpu.VMEM((heads, chunk, width), BF16),
            pltpu.VMEM((8 + tokens, pad), F32),
            pltpu.VMEM((chans, width), F32),
            pltpu.VMEM((width, chans), BF16),
            pltpu.VMEM((width, chans), BF16),
            pltpu.VMEM((tokens, chans), F32),
            pltpu.VMEM((blocks, chans, NSTATE), F32),
            pltpu.VMEM((8, 128), F32),
            pltpu.VMEM((chans, NSTATE), F32),
            pltpu.VMEM((seqs, chans + 8, NSTATE), F32),
            pltpu.VMEM((heads, groups, 128), F32),
            pltpu.VMEM((groups, 128), F32),
            sems((outs, 2)),
            sems((outs,)),
            sems((outs, ins - 1)),
            sems((outs, ins - 1)),
            sems((2,)),
            sems((2 * heads,)),
            sems,
            sems,
            sems((seqs - 1,)),
            sems((seqs - 1,)),
            sems((heads - 1,)),
            sems((heads - 1,)),
        ],
        compiler_params=pltpu.CompilerParams(
            collective_id=3, has_side_effects=True, vmem_limit_bytes=VMEM_LIMIT
        ),
        name="forward",
    )(proj, cot, out_w, conv_p, head_p, chan_p, expand)


class LineReduce:
    def __init__(self, parts, y_in, z_in, sems, seq, head, heads, partner):
        self.parts, self.y_in, self.z_in = parts, y_in, z_in
        self.y_send, self.y_recv, self.z_send, self.z_recv = sems
        self.seq, self.partner = seq, partner
        self.ins = inner_count(heads)
        self.outs = heads // self.ins
        self.at_out, self.at_in = head // self.ins, lax.rem(head, self.ins)
        self.upper = self.at_out // (self.outs // 2)
        self.mirrored = self.at_out + self.upper * (self.outs - 1 - 2 * self.at_out)

    def target(self, step):
        last = (step + 1) // self.outs
        far = self.outs - 1 - step
        far = far - (self.mirrored - far + self.outs) // self.outs
        far = far + self.upper * (self.outs - 1 - 2 * far)
        return far + last * (self.at_out - far)

    def y_copy(self, step, j):
        to = lax.rem(self.at_in + 1 + j, self.ins)
        slot = self.target(step) * (self.ins - 1) + j
        return remote(
            self.parts.at[self.target(step) * self.ins + to],
            self.y_in.at[slot],
            self.y_send.at[slot],
            self.y_recv.at[slot],
            self.seq,
            self.at_out * self.ins + to,
        )

    def give(self, make):
        @pl.loop(0, self.outs)
        def _(step):
            for j in range(self.ins - 1):
                make(self.target(step) * self.ins + lax.rem(self.at_in + 1 + j, self.ins))
                self.y_copy(step, j).start()

    def own(self, make):
        @pl.loop(0, self.outs)
        def _(step):
            make(self.target(step) * self.ins + self.at_in)

    def take(self, where, slot):
        remote(
            self.parts.at[0],
            self.z_in.at[slot],
            self.z_send.at[0],
            self.z_recv.at[slot],
            self.partner,
            self.at_out * self.ins + self.at_in,
        ).wait_recv()
        self.parts[where] = self.parts[where] + self.z_in[slot]

    def pass_on(self, where, step, up):
        slot = self.target(step) + up
        remote(
            self.parts.at[where],
            self.z_in.at[slot],
            self.z_send.at[step],
            self.z_recv.at[slot],
            self.seq,
            (self.at_out + 2 * up - 1) * self.ins + self.at_in,
        ).start()

    def reduce(self, step):
        goal = self.target(step)
        where = goal * self.ins + self.at_in
        for j in range(self.ins - 1):
            self.y_copy(step, j).wait_recv()
            self.parts[where] = self.parts[where] + self.y_in[goal * (self.ins - 1) + j]
        from_below, from_above = self.at_out > 0, self.at_out < self.outs - 1

        @pl.when((goal >= self.at_out) & from_below)
        def _():
            self.take(where, goal + 1)

        @pl.when((goal <= self.at_out) & from_above)
        def _():
            self.take(where, goal)

        if step < self.outs - 1:

            @pl.when(goal > self.at_out)
            def _():
                self.pass_on(where, step, 1)

            @pl.when(goal < self.at_out)
            def _():
                self.pass_on(where, step, 0)

    def finish(self):
        @pl.loop(0, self.outs)
        def _(step):
            for j in range(self.ins - 1):
                self.y_copy(step, j).wait_send()

        for step in range(self.outs - 1):
            remote(
                self.parts.at[0],
                self.z_in.at[0],
                self.z_send.at[step],
                self.z_recv.at[0],
                self.partner,
                self.at_out * self.ins + self.at_in,
            ).wait_send()


def backward_kernel(dims, *refs):
    seqs, heads, chunk, chans, pad = dims
    (
        proj, edge_in, cot_hi, cot_lo, conv_in, cum_in, step_in, state_in, mixed_in, cross_in,
        stat_in, out_w, resid, conv_p, head_p, chan_p, expand_in,
        result_o, gp_hi, gp_lo, out_o, wide_o, chan_o, head_o,
        pj, ngh, ngl, owh, owl, gmix, fedg, adj, run, exch, gconv,
        parts, y_in, z_in, chi, clo, oparts, keep, core_in, x_in, head_acc,
        y_send, y_recv, z_send, z_recv, load_sem, s_send, s_recv, e_send, e_recv,
        c_send, c_recv, x_send, x_recv, f_send, f_recv, o_sem,
    ) = refs
    tokens = chunk * heads
    blocks = tokens // BLOCK
    span = 2 * chans
    wide = chans + 2 * NSTATE
    half = chans // 2
    rounds = (seqs // 2).bit_length() - 1
    split_at = resid.shape[1] // 2
    seq, head = lax.axis_index("seq"), lax.axis_index("head")
    side = lax.rem(seq, 2)
    partner = seq + 1 - 2 * side
    loads = [
        pltpu.make_async_copy(a, b, load_sem.at[n])
        for n, (a, b) in enumerate(
            (
                (proj, pj.at[pl.ds(8, tokens)]),
                (edge_in, pj.at[pl.ds(0, 8)]),
                (cot_hi.at[:, pl.ds(0, split_at)], chi),
                (cot_lo.at[:, pl.ds(0, split_at)], clo),
                (out_w, oparts),
            )
        )
    ]
    for load in loads:
        load.start()
    greet(seq, head, seqs, heads)
    loads[4].wait()
    owh[...], owl[...] = halves(oparts[...])
    expand = expand_in[...]
    tri_r = lax.broadcasted_iota(jnp.int32, (BLOCK, BLOCK), 0)
    tri_c = lax.broadcasted_iota(jnp.int32, (BLOCK, BLOCK), 1)
    causal = tri_r >= tri_c
    upper = (tri_r <= tri_c).astype(F32)
    wide_o[...] = jnp.zeros_like(wide_o)
    chan_o[...] = jnp.zeros_like(chan_o)
    head_acc[...] = jnp.zeros_like(head_acc)
    run[...] = jnp.zeros_like(run)
    for load in loads[:2]:
        load.wait()
    per = BLOCK // 128
    groups = tokens // 128
    turned_stats = stat_in[...].T
    inner_total = DI_TOTAL(heads, chans)
    gain_row, skip_row = chan_p[0:1, :], chan_p[1:2, :]

    for b in range(blocks - 1, -1, -1):
        at = b * BLOCK
        here = slice(at, at + BLOCK)
        squares = jnp.concatenate(
            [turned_stats[:, b * per + n : b * per + n + 1] for n in range(per)], 0
        )
        cross = jnp.concatenate(
            [
                turned_stats[:, groups + b * per + n : groups + b * per + n + 1]
                for n in range(per)
            ],
            0,
        )
        scale = lax.rsqrt(squares / inner_total + EPSILON)
        factor = scale * scale * scale * (cross / inner_total)
        gate = pj[at + 8 : at + 8 + BLOCK, 0:chans]
        sig = logistic(gate)
        gate_act = gate * sig
        mixed = mixed_in[here, :]
        gated = mixed * gate_act
        grad_ng = cross_in[here, :]
        grad_gated = scale * (grad_ng * gain_row) - gated * factor
        scaled = gated * scale
        ngh[here, :], ngl[here, :] = halves(scaled * gain_row)
        grad_mixed = grad_gated * gate_act
        gmix[here, :] = grad_mixed
        gp_hi[here, 0:chans], gp_lo[here, 0:chans] = halves(
            grad_gated * mixed * (sig * (1.0 + gate * (1.0 - sig)))
        )
        conv = conv_in[here, :]
        act = conv * logistic(conv)
        chan_o[0:1, :] = chan_o[0:1, :] + jnp.sum(grad_ng * scaled, 0, keepdims=True)
        chan_o[1:2, :] = chan_o[1:2, :] + jnp.sum(grad_mixed * act[:, :chans], 0, keepdims=True)
        early = grad_mixed * dotx(jnp.exp(cum_in[here, :]), expand, 1, 0)
        adj[b] = run[...]
        run[...] = row_scale(cum_in[at + BLOCK - 1 : at + BLOCK, :], expand) * run[...] + dotx(
            early, act[:, chans + NSTATE :], 0, 0
        )
        gconv[here, chans + NSTATE :] = dotx(early, state_in[b], 1, 0)

    total = jnp.zeros((1, 128), F32)
    for b in range(blocks):
        total = total + cum_in[(b + 1) * BLOCK - 1 : (b + 1) * BLOCK, :]
    exch[seq, 0:chans, :] = run[...]
    exch[seq, chans : chans + 8, :] = jnp.broadcast_to(total, (8, 128))

    def state_copy(at, j, to):
        return remote(exch.at[at], exch.at[at], s_send.at[j - 1], s_recv.at[j - 1], to, head)

    for j in range(1, seqs):

        @pl.when(seq - j >= 0)
        def _():
            state_copy(seq, j, seq - j).start()

    reduce = LineReduce(
        parts, y_in, z_in, (y_send, y_recv, z_send, z_recv), seq, head, heads, partner
    )

    def product_chunk(where):
        rows = pl.ds(pl.multiple_of(where * chunk, 8), chunk)
        parts[where] = dot3((ngh[rows, :], ngl[rows, :]), (owh[...], owl[...]), 1, 0)

    reduce.give(product_chunk)
    for load in loads[2:4]:
        load.wait()
    oparts[:, :split_at] = dot3((ngh[...], ngl[...]), (chi[...], clo[...]), 0, 0)
    rest = [
        pltpu.make_async_copy(a.at[:, pl.ds(split_at, split_at)], b, load_sem.at[n])
        for n, (a, b) in enumerate(((cot_hi, chi), (cot_lo, clo)))
    ]
    for load in rest:
        load.start()
    reduce.own(product_chunk)
    for load in rest:
        load.wait()
    oparts[:, split_at:] = dot3((ngh[...], ngl[...]), (chi[...], clo[...]), 0, 0)
    mine = pl.ds(pl.multiple_of(side * half, 8), half)
    theirs = pl.ds(pl.multiple_of((1 - side) * half, 8), half)
    keep[...] = oparts[mine, :]
    core = remote(oparts.at[theirs], core_in, c_send, c_recv, partner, head)
    core.start()

    @pl.loop(0, blocks)
    def _(b):
        at = pl.multiple_of(b * BLOCK, BLOCK)
        here = pl.ds(at, BLOCK)
        conv = conv_in[here, :]
        act = conv * logistic(conv)
        writes, reads = act[:, chans : chans + NSTATE], act[:, chans + NSTATE :]
        scores = dotx(reads, writes, 1, 1)
        cum = cum_in[here, :]
        turned = cum.T
        fed_all = act[:, :chans] * dotx(step_in[here, :], expand, 1, 0)
        grad_scores = jnp.zeros((BLOCK, BLOCK), F32)
        for first_lane, end in lanes_of(chans):
            fed = fed_all[:, first_lane:end]
            grad = gmix[here, first_lane:end]
            lane = lax.broadcasted_iota(jnp.int32, fed.shape, 1)
            outs = []
            for start in range(first_lane, end, HEADDIM):
                decay = decay_of(cum, turned, start // HEADDIM, causal)
                inside = (lane // HEADDIM) == (start - first_lane) // HEADDIM
                grad_scores = grad_scores + decay * dotx(jnp.where(inside, grad, 0.0), fed, 1, 1)
                outs.append(dotx(decay * scores, grad, 0, 0))
            out = outs[0]
            if len(outs) == 2:
                out = jnp.where(lane < HEADDIM, outs[0], outs[1])
            fedg[here, first_lane:end] = out
        gconv[here, chans : chans + NSTATE] = dotx(grad_scores, reads, 0, 0)
        gconv[here, chans + NSTATE :] = gconv[here, chans + NSTATE :] + dotx(grad_scores, writes, 1, 0)

    core.wait()
    keep[...] = keep[...] + core_in[...]
    x_copies = []

    def x_start(source, turn):
        far = seq + (2 << turn) - 2 * (2 << turn) * lax.rem(seq // (2 << turn), 2)
        x_copies.append(
            remote(source, x_in.at[turn], x_send.at[turn], x_recv.at[turn], far, head)
        )
        x_copies[-1].start()

    x_start(keep, 0)
    reduce.reduce(0)
    run[...] = jnp.zeros_like(run)
    for back in range(seqs - 1):
        later = seqs - 1 - back

        @pl.when(later > seq)
        def _():
            for j in range(1, seqs):

                @pl.when(later - seq == j)
                def _():
                    state_copy(later, j, partner).wait_recv()

            run[...] = (
                row_scale(exch[later, chans : chans + 1, :], expand) * run[...]
                + exch[later, 0:chans, :]
            )

    for b in range(blocks - 1, -1, -1):
        adj[b] = adj[b] + run[...]
        run[...] = row_scale(cum_in[(b + 1) * BLOCK - 1 : (b + 1) * BLOCK, :], expand) * run[...]

    lane_ones = jnp.ones((8, NSTATE), F32)

    @pl.loop(0, blocks)
    def _(b):
        at = pl.multiple_of(b * BLOCK, BLOCK)
        here = pl.ds(at, BLOCK)
        conv = conv_in[here, :]
        sig = logistic(conv)
        act = conv * sig
        slope = sig * (1.0 + conv * (1.0 - sig))
        inner, writes = act[:, :chans], act[:, chans : chans + NSTATE]
        cum = cum_in[here, :]
        step = step_in[here, :]
        last = cum[BLOCK - 1 : BLOCK, :]
        step_wide = dotx(step, expand, 1, 0)
        tails = dotx(jnp.exp(last - cum), expand, 1, 0)
        fed = inner * step_wide
        grad_state = adj[b]
        from_state = tails * dotx(writes, grad_state, 1, 1)
        grad_fed = fedg[here, :] + from_state
        grad_mixed = gmix[here, :]
        grad_writes = gconv[here, chans : chans + NSTATE] + dotx(fed * tails, grad_state, 1, 0)
        direct = dotx(inner * grad_fed, expand, 1, 1)
        scanned = mixed_in[here, :] - skip_row * inner
        grad_cum = dotx(grad_mixed * scanned - fed * grad_fed, expand, 1, 1)
        kept = dotx(expand, grad_state * state_in[b], 1, 0)
        kept = dotx(lane_ones, kept, 1, 1)[0:1, :] * jnp.exp(last)
        grad_last = kept + jnp.sum(dotx(fed * from_state, expand, 1, 1), 0, keepdims=True)
        grad_log = dotx(upper, grad_cum, 1, 0) + grad_last
        rate = head_p[1:2, :]
        head_acc[1:2, :] = head_acc[1:2, :] + jnp.sum(step * grad_log, 0, keepdims=True) * rate
        arg = pj[pl.ds(at + 8, BLOCK), span + 2 * NSTATE : pad] + head_p[0:1, :]
        grad_arg = (direct + rate * grad_log) * logistic(arg) * head_p[2:3, :]
        head_acc[0:1, :] = head_acc[0:1, :] + jnp.sum(grad_arg, 0, keepdims=True)
        gp_hi[here, span + 2 * NSTATE : pad], gp_lo[here, span + 2 * NSTATE : pad] = halves(
            grad_arg
        )
        gconv[here, 0:chans] = (step_wide * grad_fed + skip_row * grad_mixed) * slope[:, :chans]
        gconv[here, chans : chans + NSTATE] = grad_writes * slope[:, chans : chans + NSTATE]
        gconv[here, chans + NSTATE :] = gconv[here, chans + NSTATE :] * slope[:, chans + NSTATE :]

    reduce.reduce(1)
    edge = remote(
        gconv.at[pl.ds(0, 8)],
        gconv.at[pl.ds(tokens, 8)],
        e_send,
        e_recv,
        lax.rem(seq + seqs - 1, seqs),
        head,
    )
    edge.start()
    head_o[...] = head_acc[...]

    def conv_back(b):
        at = pl.multiple_of(b * BLOCK, BLOCK)
        here = pl.ds(at, BLOCK)
        window = pj[pl.ds(at, BLOCK + 8), chans : span + 2 * NSTATE]
        ahead = gconv[pl.ds(at, BLOCK + 8), :]
        grad = ahead[0:BLOCK, :]
        grad_pre = jnp.zeros((BLOCK, wide), F32)
        for k in range(WIDTH):
            grad_pre = grad_pre + conv_p[k : k + 1, :] * ahead[3 - k : 3 - k + BLOCK, :]
            wide_o[k : k + 1, :] = wide_o[k : k + 1, :] + jnp.sum(
                grad * window[5 + k : 5 + k + BLOCK, :], 0, keepdims=True
            )
        wide_o[4:5, :] = wide_o[4:5, :] + jnp.sum(grad, 0, keepdims=True)
        (
            gp_hi[here, chans : span + 2 * NSTATE],
            gp_lo[here, chans : span + 2 * NSTATE],
        ) = halves(grad_pre)

    @pl.loop(0, blocks - 1)
    def _(b):
        conv_back(b)

    edge.wait()
    gconv[tokens : tokens + 8, :] = jnp.where(seq < seqs - 1, gconv[tokens : tokens + 8, :], 0.0)

    @pl.loop(blocks - 1, blocks)
    def _(b):
        conv_back(b)

    for step in range(2, reduce.outs - 1):
        reduce.reduce(step)
    now, new = keep, core_in
    for turn in range(rounds):
        x_copies[turn].wait()
        new[...] = now[...] + x_in[turn]
        now, new = new, now
        if turn + 1 < rounds:
            x_start(now, turn + 1)
    put = pltpu.make_async_copy(now, out_o.at[mine], o_sem)
    put.start()
    final = remote(now, out_o.at[mine], f_send, f_recv, partner, head)
    final.start()
    reduce.reduce(reduce.outs - 1)
    result_o[...] = resid[...] + parts[head]
    reduce.finish()
    for j in range(1, seqs):

        @pl.when(seq - j >= 0)
        def _():
            state_copy(seq, j, seq - j).wait_send()

    final.wait_send()
    remote(now, out_o.at[theirs], f_send, f_recv, partner, head).wait_recv()
    put.wait()


def DI_TOTAL(heads, chans):
    return float(heads * chans)


def backward(proj, kept, out_w, resid, conv_p, head_p, chan_p, expand, seqs, heads):
    (cot_hi, cot_lo, conv, cum, step, state, mixed, cross, stat, edge) = kept
    tokens, pad = proj.shape
    chunk, width = resid.shape
    chans = out_w.shape[0]
    ins = inner_count(heads)
    outs = heads // ins
    wide = chans + 2 * NSTATE
    blocks = tokens // BLOCK
    half = chans // 2
    rounds = (seqs // 2).bit_length() - 1
    anywhere = pl.BlockSpec(memory_space=pl.ANY)
    local = pl.BlockSpec(memory_space=pltpu.VMEM)
    sems = pltpu.SemaphoreType.DMA
    shape = jax.ShapeDtypeStruct
    return pl.pallas_call(
        functools.partial(backward_kernel, (seqs, heads, chunk, chans, pad)),
        out_shape=(
            shape((chunk, width), F32),
            shape((tokens, pad), BF16),
            shape((tokens, pad), BF16),
            shape((chans, width), F32),
            shape((8, wide), F32),
            shape((8, chans), F32),
            shape((8, 128), F32),
        ),
        in_specs=[anywhere] * 4 + [local] * 7 + [anywhere] + [local] * 5,
        out_specs=(local, local, local, anywhere, local, local, local),
        scratch_shapes=[
            pltpu.VMEM((8 + tokens, pad), F32),
            pltpu.VMEM((tokens, chans), BF16),
            pltpu.VMEM((tokens, chans), BF16),
            pltpu.VMEM((chans, width), BF16),
            pltpu.VMEM((chans, width), BF16),
            pltpu.VMEM((tokens, chans), F32),
            pltpu.VMEM((tokens, chans), F32),
            pltpu.VMEM((blocks, chans, NSTATE), F32),
            pltpu.VMEM((chans, NSTATE), F32),
            pltpu.VMEM((seqs, chans + 8, NSTATE), F32),
            pltpu.VMEM((tokens + 8, wide), F32),
            pltpu.VMEM((heads, chunk, width), F32),
            pltpu.VMEM((outs * (ins - 1), chunk, width), F32),
            pltpu.VMEM((outs + 1, chunk, width), F32),
            pltpu.VMEM((tokens, width // 2), BF16),
            pltpu.VMEM((tokens, width // 2), BF16),
            pltpu.VMEM((chans, width), F32),
            pltpu.VMEM((half, width), F32),
            pltpu.VMEM((half, width), F32),
            pltpu.VMEM((rounds, half, width), F32),
            pltpu.VMEM((8, 128), F32),
            sems((outs * (ins - 1),)),
            sems((outs * (ins - 1),)),
            sems((outs,)),
            sems((outs + 1,)),
            sems((5,)),
            sems((seqs - 1,)),
            sems((seqs - 1,)),
            sems,
            sems,
            sems,
            sems,
            sems((rounds,)),
            sems((rounds,)),
            sems,
            sems,
            sems,
        ],
        compiler_params=pltpu.CompilerParams(
            collective_id=4, has_side_effects=True, vmem_limit_bytes=VMEM_LIMIT
        ),
        name="backward",
    )(
        proj, edge, cot_hi, cot_lo, conv, cum, step, state, mixed, cross, stat,
        out_w, resid, conv_p, head_p, chan_p, expand,
    )


def on_device(
    residual_in,
    norm_gain,
    gate_weight,
    inner_weight,
    bc_weight,
    step_weight,
    conv_inner_weight,
    conv_inner_bias,
    conv_bc_weight,
    conv_bc_bias,
    step_bias,
    decay_log,
    skip_gain,
    gated_gain,
    out_weight,
    cotangent,
):
    seqs, heads = lax.axis_size("seq"), lax.axis_size("head")
    width = residual_in.shape[2]
    chans = gate_weight.shape[0]
    heads_here = step_weight.shape[0]
    spare = 128 - heads_here
    resid = residual_in.reshape(-1, width)
    cot = cotangent.reshape(-1, width)
    gain = norm_gain.reshape(1, width)

    def eight(part):
        return jnp.pad(part, ((0, 8 - part.shape[0]), (0, 0)))

    def by_head(*parts):
        return eight(jnp.pad(jnp.stack(parts), ((0, 0), (0, spare))))

    conv_p = eight(
        jnp.concatenate(
            [
                jnp.concatenate([conv_inner_weight, conv_bc_weight], 1),
                jnp.concatenate([conv_inner_bias, conv_bc_bias])[None],
            ],
            0,
        )
    )
    head_p = by_head(step_bias, -jnp.exp(decay_log), jnp.ones_like(step_bias))
    chan_p = eight(jnp.stack([gated_gain, jnp.repeat(skip_gain, HEADDIM)]))
    expand = (
        lax.broadcasted_iota(jnp.int32, (128, chans), 0)
        == lax.broadcasted_iota(jnp.int32, (128, chans), 1) // HEADDIM
    ).astype(F32)
    hat_hi, hat_lo, projected, weight_hi, weight_lo = gather_project(
        resid,
        gain,
        gate_weight,
        inner_weight,
        bc_weight,
        jnp.pad(step_weight, ((0, spare), (0, 0))),
        heads,
    )
    kept = forward(projected, cot, out_weight, conv_p, head_p, chan_p, expand, seqs, heads)
    result, grad_hi, grad_lo, out_weight_grad, wide_sums, chan_sums, head_sums = backward(
        projected, kept, out_weight, resid, conv_p, head_p, chan_p, expand, seqs, heads
    )

    def packed(*parts):
        flat = jnp.concatenate([part.reshape(-1) for part in parts])
        count = -(-flat.shape[0] // width)
        return jnp.pad(flat, (0, count * width - flat.shape[0])).reshape(count, width)

    seq_small = packed(
        wide_sums[:WIDTH, :chans],
        wide_sums[WIDTH, :chans],
        chan_sums[0],
        head_sums[0, :heads_here],
        head_sums[1, :heads_here],
        jnp.sum(chan_sums[1].reshape(heads_here, HEADDIM), axis=1),
    )
    all_small = packed(wide_sums[: WIDTH + 1, chans:])
    small = jnp.stack(
        [
            jnp.zeros((8, width), F32),
            eight(seq_small),
            eight(jnp.concatenate([jnp.zeros((1, width), F32), all_small], 0)),
        ]
    )
    residual_grad, gate_weight_grad, inner_weight_grad, bc_pieces, sums = tail(
        (grad_hi, grad_lo),
        (hat_hi, hat_lo),
        (weight_hi, weight_lo),
        small,
        resid,
        cot,
        gain,
        seqs,
        heads,
        chans,
    )
    across = width // bc_pieces.shape[2]
    bc_weight_grad = jnp.transpose(
        bc_pieces.reshape(2 * NSTATE // 8, across, 8, width // across), (1, 3, 0, 2)
    ).reshape(width, 2 * NSTATE)
    flat = sums[1].reshape(-1)

    def take(count):
        nonlocal flat
        first, flat = flat[:count], flat[count:]
        return first

    conv_inner_weight_grad = take(WIDTH * chans).reshape(WIDTH, chans)
    conv_inner_bias_grad = take(chans)
    gated_gain_grad = take(chans)
    step_bias_grad = take(heads_here)
    decay_log_grad = take(heads_here)
    skip_gain_grad = take(heads_here)
    flat = sums[2, 1:].reshape(-1)
    conv_bc_weight_grad = take(WIDTH * 2 * NSTATE).reshape(WIDTH, 2 * NSTATE)
    conv_bc_bias_grad = take(2 * NSTATE)
    return (
        result.reshape(residual_in.shape),
        residual_grad.reshape(residual_in.shape),
        sums[2, 0],
        gate_weight_grad,
        inner_weight_grad,
        bc_weight_grad,
        sums[0, :heads_here],
        conv_inner_weight_grad,
        conv_inner_bias_grad,
        conv_bc_weight_grad,
        conv_bc_bias_grad,
        step_bias_grad,
        decay_log_grad,
        skip_gain_grad,
        gated_gain_grad,
        out_weight_grad,
    )


def solution(mesh):
    placed = (
        P(None, ("seq", "head"), None),
        P(),
        P("head", None),
        P("head", None),
        P(),
        P("head", None),
        P(None, "head"),
        P("head"),
        P(),
        P(),
        P("head"),
        P("head"),
        P("head"),
        P("head"),
        P("head", None),
        P(None, ("seq", "head"), None),
    )
    return jax.shard_map(
        on_device,
        mesh=mesh,
        in_specs=placed,
        out_specs=(
            P(None, ("seq", "head"), None),
            P(None, ("seq", "head"), None),
            P(),
            P("head", None),
            P("head", None),
            P(),
            P("head", None),
            P(None, "head"),
            P("head"),
            P(),
            P(),
            P("head"),
            P("head"),
            P("head"),
            P("head"),
            P("head", None),
        ),
        check_vma=False,
    )
```

time: 921 us -> 442 us (0.48)
  waiting for transfers between devices: 479 us -> 0 us
  Pallas kernels: 0 us -> 407 us
  matrix products: 168 us -> 0 us
  blocking collectives: 112 us -> 0 us
  other arithmetic: 67.9 us -> 2.88 us
  local copies, waits for them, and re-layouts: 65.5 us -> 24.6 us
  between operations: 16.6 us -> 1.01 us
    pallas_call x0 -> x4, Pallas kernels: none -> 407 us  [the longest x1 139 us: tail(): pl.pallas_call(functools.partial(tail_kernel, (seqs, heads, chunk, chans,...]
    psum x2 -> x0, waiting for transfers between devices: 192 us -> none  [the longest x1 115 us: on_device(): lax.psum((norm_gain_grad, gate_weight_grad, inner_weight_grad, bc_weight_...]
    reduce_scatter x2 -> x0, waiting for transfers between devices: 189 us -> none  [the longest x1 119 us: on_device(): lax.psum_scatter(grad_normed_part, 'head', scatter_dimension=1, tiled=True)]
    dot_general x20 -> x0, matrix products: 168 us -> none  [the longest x2 43.1 us: product(): jnp.dot(left_side, right_side, precision=HIGH, preferred_element_type=jnp...]
    all_gather x2 -> x0, waiting for transfers between devices: 95.8 us -> none  [the longest x1 95.8 us: on_device(): rows = lax.all_gather(residual_in, 'head', axis=1, tiled=True)]
    psum x4 -> x0, blocking collectives: 87.2 us -> none  [the longest x1 37.1 us: on_device(): lax.psum((gain_part, bc_part, conv_bc_part, conv_bias_part), 'head')]
    reduce_sum x12 -> x1, other arithmetic: 25.5 us -> 0.12 us  [on_device(): jnp.sum(chan_sums[1].reshape(heads_here, HEADDIM), axis=1)]
    all_gather x2 -> x0, blocking collectives: 18 us -> none  [entering_2(): everything = jax.tree.map(lambda part: lax.all_gather(part, axis), x)]
  transfers between devices with their start and end apart: 8 -> 0, of which waited for: 6 -> 0; matrix products, arithmetic and copies ran while one was open for 17% -> 0% of each run, Pallas kernels for 0% -> 0%
where the time goes in v1:
time: 442 us; the launch traced here: 435 us
  Pallas kernels  407 us (92%)
  local copies, waits for them, and re-layouts  24.6 us (6%)
    pallas_call x1, Pallas kernels, tail(): pl.pallas_call(functools.partial(tail_kernel, (seqs, heads, chunk, chans,...  139 us
    pallas_call x1, Pallas kernels, backward(): pl.pallas_call(functools.partial(backward_kernel, (seqs, heads, chunk, ch...  101 us
    pallas_call x1, Pallas kernels, forward(): pl.pallas_call(functools.partial(forward_kernel, (seqs, heads, chunk, cha...  85.9 us
    pallas_call x1, Pallas kernels, gather_project(): pl.pallas_call(functools.partial(head_kernel, (heads, chunk, chans, pad))...  80.6 us
    unnamed x32, local copies, waits for them, and re-layouts  12.5 us

profile of v1, /device:TPU:0, one launch (start us, length us, event | category | flops | bytes accessed | tf_op | source)
XLA Modules:
  0.0 435.4 jit_solution(11565187430879154072)
XLA Ops:
  0.6 1.3 reshape.75.refs_1_.refs_9_
  1.9 1.8 pad.36.refs_5_
  3.7 0.0 copy-start.10
  3.7 0.0 copy-start.8
  3.7 0.0 copy-start.12
  3.7 0.0 copy-start.11
  3.8 80.6 %gather_project.1 = (bf16[1024,1536]{1,0:T(8,128)(2,1)}, bf16[1024,1536]{1,0:T(8,128)(2,1)}, f32[1024,1152]{1,0:T(8,128)}, bf16[1152,1536]{1,0:T(8,128)(2,1)}, bf16[1152,1536]{1,0:T(8,128)(2,1)}) custom-call(f32[128,1536]{1,0:T(8,128)} %bitcast.24, f32[1,1536]{1,0:T(1,128)} %reshape.75.refs_1_.refs_9_, f32[384,1536]{1,0:T(8,128)} %refs_2_.2, ...), custom_call_target="tpu_custom_call" | custom-call | tf_op jit(solution)/shard_map/gather_project/pallas_call | solution.py:691
  84.3 0.7 fusion.refs_6_.refs_16_
  85.0 0.0 copy-done.7
  85.0 0.0 copy-done.9
  85.1 0.0 copy-done.5
  85.1 0.0 copy-done.6
  85.1 0.6 select_maximum_fusion.refs_3_.refs_13_
  85.7 0.1 broadcast_in_dim.8
  85.8 0.1 stack_reshape.3
  85.9 0.0 copy-done.8
  85.9 0.6 select_maximum_fusion.2.refs_5_.refs_15_
  86.5 0.1 pad.52.clone
  86.6 0.1 maximum_maximum_fusion
  86.6 0.6 pad.61.refs_4_.refs_14_
  87.2 85.9 %forward.1 = (bf16[1024,1536]{1,0:T(8,128)(2,1)}, bf16[1024,1536]{1,0:T(8,128)(2,1)}, f32[1024,640]{1,0:T(8,128)}, f32[1024,128]{1,0:T(8,128)}, f32[1024,128]{1,...) custom-call(f32[1024,1152]{1,0:T(8,128)} %get-tuple-element.43.refs_, ...), custom_call_target="tpu_custom_call" | custom-call | tf_op jit(solution)/shard_map/forward/pallas_call | solution.py:1079
  173.2 101.1 %backward.1 = (f32[128,1536]{1,0:T(8,128)}, bf16[1024,1152]{1,0:T(8,128)(2,1)}, bf16[1024,1152]{1,0:T(8,128)(2,1)}, f32[384,1536]{1,0:T(8,128)}, f32[8,640]{1,0:...) custom-call(f32[1024,1152]{1,0:T(8,128)} %get-tuple-element.43.refs_0_, f32[8,1152]{1,0:T(8,128)} %get-tuple-element.44.refs_1_, ...), custom_call_target="tpu_custom_call" | custom-call | tf_op jit(solution)/shard_map/backward/pallas_call | solution.py:1566
  274.3 0.7 slice.80
  275.0 0.8 slice_reduce_fusion.2
  275.8 0.1 reshape_squeeze.7
  275.9 0.1 reduce_sum.9
  276.0 0.7 slice_reduce_fusion.4
  276.7 0.8 slice_bitcast_fusion.1
  277.5 0.1 concatenate.18
  277.6 0.7 slice.86
  278.3 0.7 pad_maximum_fusion.refs_6_
  279.1 139.4 %tail.1 = (f32[128,1536]{1,0:T(8,128)}, f32[384,1536]{1,0:T(8,128)}, f32[384,1536]{1,0:T(8,128)}, f32[32,8,1536]{2,1,0:T(8,128)}, f32[3,8,1536]{2,1,0:T(8,128)}) custom-call(bf16[1024,1152]{1,0:T(8,128)(2,1)} %get-tuple-element.55.refs_0_, bf16[1024,1152]{1,0:T(8,128)(2,1)} %get-tuple-element.56.refs_1_, bf16[1024,1536]{1,0:T(8,128)(2,1)} %get-tuple-element.57.refs_2_, ...), custom_call_target="tpu_custom_call" | custom-call | tf_op jit(solution)/shard_map/tail/pallas_call | solution.py:453
  418.5 3.1 copy.33
  421.7 0.6 slice.102
  422.3 0.6 fusion.5
  422.8 0.6 fusion.6
  423.4 0.6 slice.103
  424.0 0.6 slice_bitcast_fusion
  424.6 0.6 slice_reduce_fusion
  425.3 0.6 reshape.85
  425.9 0.9 copy.39
  426.7 2.1 copy.40
  428.8 0.0 copy-done.2
  428.8 1.4 copy.41
  430.2 1.1 copy-done.1
  431.3 1.4 copy.42
  432.7 1.1 copy-done
  433.9 1.4 copy.43
  (33 shorter events, 0.2 us)
Async XLA Ops:
  3.7 81.4 %copy-start.7 = (f32[384]{0:T(512)S(1)}, f32[384]{0:T(512)}, u32[]{:S(2)}) copy-start(f32[384]{0:T(512)} %param.23) | copy-start | bytes 4612
  3.7 81.4 %copy-start.9 = (f32[256]{0:T(256)S(1)}, f32[256]{0:T(256)}, u32[]{:S(2)}) copy-start(f32[256]{0:T(256)} %param.25) | copy-start | bytes 3076
  3.7 81.4 %copy-start.5 = (f32[4,384]{1,0:T(4,128)S(1)}, f32[4,384]{1,0:T(4,128)}, u32[]{:S(2)}) copy-start(f32[4,384]{1,0:T(4,128)} %param.22) | copy-start | bytes 18436
  3.7 81.4 %copy-start.6 = (f32[4,256]{1,0:T(4,128)S(1)}, f32[4,256]{1,0:T(4,128)}, u32[]{:S(2)}) copy-start(f32[4,256]{1,0:T(4,128)} %param.24) | copy-start | bytes 12292
  3.7 82.0 %copy-start.10 = (f32[6]{0:T(128)S(1)}, f32[6]{0:T(128)}, u32[]{:S(2)}) copy-start(f32[6]{0:T(128)} %param.28) | copy-start | bytes 76
  3.7 82.1 %copy-start.8 = (f32[384]{0:T(512)S(1)}, f32[384]{0:T(512)}, u32[]{:S(2)}) copy-start(f32[384]{0:T(512)} %param.29) | copy-start | bytes 4612
  3.7 82.8 %copy-start.12 = (f32[6]{0:T(128)S(1)}, f32[6]{0:T(128)}, u32[]{:S(2)}) copy-start(f32[6]{0:T(128)} %param.27) | copy-start | bytes 76
  3.7 82.8 %copy-start.11 = (f32[6]{0:T(128)S(1)}, f32[6]{0:T(128)}, u32[]{:S(2)}) copy-start(f32[6]{0:T(128)} %param.26) | copy-start | bytes 76
  418.5 3.1 copy-start.4
  418.5 7.4 %copy-start.3 = (f32[128,1536]{1,0:T(8,128)S(1)}, f32[128,1536]{1,0:T(8,128)}, u32[]{:S(2)}) copy-start(f32[128,1536]{1,0:T(8,128)} %get-tuple-element.54) | copy-start | bytes 2359300
  421.6 7.2 %copy-start.2 = (f32[384,1536]{1,0:T(8,128)S(1)}, f32[384,1536]{1,0:T(8,128)}, u32[]{:S(2)}) copy-start(f32[384,1536]{1,0:T(8,128)} %get-tuple-element.136) | copy-start | bytes 7077892
  428.8 2.5 copy-start.1
  431.3 2.5 copy-start

commit v2 on v1

--- a/solution.py
+++ b/solution.py
@@ -53,28 +53,107 @@
     return 2 if heads <= 8 else 4
 
 
+class SeqSum:
+    def __init__(self, source, base, keep, core_in, x_in, sems, result, seq, head, seqs):
+        self.source, self.base, self.keep, self.core_in, self.x_in = source, base, keep, core_in, x_in
+        self.sems, self.result, self.seq, self.head = sems, result, seq, head
+        self.rounds = (seqs // 2).bit_length() - 1
+        self.half = keep.shape[0]
+        self.side = lax.rem(seq, 2)
+        self.partner = seq + 1 - 2 * self.side
+        self.crossing = []
+
+    def rows(self, side, base):
+        return pl.ds(pl.multiple_of(base + side * self.half, 8), self.half)
+
+    def begin(self):
+        self.keep[...] = self.source[self.rows(self.side, self.base), :]
+        self.core = remote(
+            self.source.at[self.rows(1 - self.side, self.base)],
+            self.core_in,
+            self.sems.at[0],
+            self.sems.at[1],
+            self.partner,
+            self.head,
+        )
+        self.core.start()
+
+    def cross(self, source, turn):
+        away = 2 << turn
+        far = self.seq + away - 2 * away * lax.rem(self.seq // away, 2)
+        self.crossing.append(
+            remote(
+                source,
+                self.x_in.at[turn],
+                self.sems.at[5 + 2 * turn],
+                self.sems.at[6 + 2 * turn],
+                far,
+                self.head,
+            )
+        )
+        self.crossing[-1].start()
+
+    def pair(self):
+        self.core.wait()
+        self.keep[...] = self.keep[...] + self.core_in[...]
+        self.cross(self.keep, 0)
+
+    def total(self):
+        now, new = self.keep, self.core_in
+        for turn in range(self.rounds):
+            self.crossing[turn].wait()
+            new[...] = now[...] + self.x_in[turn]
+            now, new = new, now
+            if turn + 1 < self.rounds:
+                self.cross(now, turn + 1)
+        mine = self.result.at[self.rows(self.side, 0)]
+        self.now = now
+        self.put = pltpu.make_async_copy(now, mine, self.sems.at[2])
+        self.put.start()
+        self.final = remote(
+            now, mine, self.sems.at[3], self.sems.at[4], self.partner, self.head
+        )
+        self.final.start()
+
+    def end(self):
+        self.final.wait_send()
+        remote(
+            self.now,
+            self.result.at[self.rows(1 - self.side, 0)],
+            self.sems.at[3],
+            self.sems.at[4],
+            self.partner,
+            self.head,
+        ).wait_recv()
+        self.put.wait()
+
+
+def seq_sum_scratch(half, width, rounds):
+    return [
+        pltpu.VMEM((half, width), F32),
+        pltpu.VMEM((half, width), F32),
+        pltpu.VMEM((rounds, half, width), F32),
+        pltpu.SemaphoreType.DMA((5 + 2 * rounds,)),
+    ]
+
+
 def tail_kernel(dims, *refs):
     seqs, heads, chunk, chans, pad = dims
     (
         gp_hi, gp_lo, hat_hi, hat_lo, w_hi, w_lo, small_in, resid, cot, gain,
-        resid_grad, gate_out, inner_out, bc_out, small_out,
-        gph, gpl, hth, htl, wh, wl, grads, y_in, z_in, joined, keep, core_in, x_in,
-        bc_part, bc_seq, bc_head, bc_full, small_all, small_head,
-        load_sem, y_send, y_recv, z_send, z_recv, c_send, c_recv, x_send, x_recv,
-        f_send, f_recv, o_sem, ba_s, ba_r, bb_s, bb_r, bc_s, bc_r, bd_s, bd_r,
-        sa_s, sa_r, sb_s, sb_r,
+        resid_grad, inner_out, bc_out, small_out,
+        gph, gpl, hth, htl, wh, wl, parts, y_in, z_in, joined, keep, core_in, x_in, i_sems,
+        bc_part, bc_half, bc_seq, bc_quart, bc_head, bc_full,
+        small_mine, small_pair, small_far, small_head,
+        load_sem, y_send, y_recv, z_send, z_recv,
+        a_sem, b_send, b_recv, c_send, c_recv, m_sem, h_send, h_recv, put_sem,
     ) = refs
     width = gain.shape[1]
-    ins = inner_count(heads)
-    outs = heads // ins
-    rounds = (seqs // 2).bit_length() - 1
-    half = chans // 2
     span = 2 * chans
+    fars = seqs // 2
     seq, head = lax.axis_index("seq"), lax.axis_index("head")
-    at_out, at_in = head // ins, lax.rem(head, ins)
-    side = lax.rem(seq, 2)
+    side, far = lax.rem(seq, 2), seq // 2
     partner = seq + 1 - 2 * side
-
     loads = [
         pltpu.make_async_copy(a, b, load_sem.at[n])
         for n, (a, b) in enumerate(
@@ -83,356 +162,223 @@
     ]
     for load in loads:
         load.start()
-    mine = pl.ds(pl.multiple_of(side * half, 8), half)
-    theirs = pl.ds(pl.multiple_of((1 - side) * half, 8), half)
     greet(seq, head, seqs, heads)
-
-    core = [None] * 2
+    reduce = LineReduce(
+        parts, y_in, z_in, (y_send, y_recv, z_send, z_recv), seq, head, heads, partner
+    )
     for load in loads[:4]:
         load.wait()
 
-    upper = at_out // (outs // 2)
-    mirrored = at_out + upper * (outs - 1 - 2 * at_out)
-
-    def target(step):
-        last = (step + 1) // outs
-        far = outs - 1 - step
-        far = far - (mirrored - far + outs) // outs
-        far = far + upper * (outs - 1 - 2 * far)
-        return far + last * (at_out - far)
-
-    def chunk_grad(step, inside):
-        where = target(step) * ins + inside
-        rows = pl.ds(pl.multiple_of(where * chunk, 8), chunk)
-        grads[where] = dot3((gph[rows, :], gpl[rows, :]), (wh[...], wl[...]), 1, 0)
-        return where
-
-    def y_copy(step, j):
-        to = lax.rem(at_in + 1 + j, ins)
-        where = target(step) * ins + to
-        slot = target(step) * (ins - 1) + j
-        return remote(
-            grads.at[where],
-            y_in.at[slot],
-            y_send.at[slot],
-            y_recv.at[slot],
-            seq,
-            at_out * ins + to,
-        )
-
-    @pl.loop(0, outs)
-    def _(step):
-        for j in range(ins - 1):
-            chunk_grad(step, lax.rem(at_in + 1 + j, ins))
-            y_copy(step, j).start()
-
-    x_copies = {}
-
-    def x_start(n, source, turn):
-        far = seq + (2 << turn) - 2 * (2 << turn) * lax.rem(seq // (2 << turn), 2)
-        x_copies[n, turn] = remote(
-            source, x_in.at[n, turn], x_send.at[n, turn], x_recv.at[n, turn], far, head
-        )
-        x_copies[n, turn].start()
-
-    def after_core(n):
-        core[n].wait()
-        keep[n] = keep[n] + core_in[n]
-        x_start(n, keep.at[n], 0)
-
-    finals = {}
-    puts = {}
-
-    def after_x(n, result):
-        now, new = keep, core_in
-        for turn in range(rounds):
-            x_copies[n, turn].wait()
-            new[n] = now[n] + x_in[n, turn]
-            now, new = new, now
-            if turn + 1 < rounds:
-                x_start(n, now.at[n], turn + 1)
-        puts[n] = pltpu.make_async_copy(now.at[n], result.at[mine], o_sem.at[n])
-        puts[n].start()
-        finals[n] = remote(
-            now.at[n], result.at[mine], f_send.at[n], f_recv.at[n], partner, head
-        )
-        finals[n].start()
-
+    def chunk_rows(where):
+        return pl.ds(pl.multiple_of(where * chunk, 8), chunk)
+
+    ins = reduce.ins
+
+    def produce(step):
+        first = reduce.target(step) * ins
+        rows = pl.ds(pl.multiple_of(first * chunk, 8), ins * chunk)
+        out = dot3((gph[rows, :], gpl[rows, :]), (wh[...], wl[...]), 1, 0)
+        for n in range(ins):
+            parts[first + n] = out[n * chunk : (n + 1) * chunk]
+
+    produce(jnp.int32(0))
+    reduce.give(jnp.int32(0))
+    reduce.give(jnp.int32(1))
+    gain_row = gain[...]
     for load in loads[4:]:
         load.wait()
-    joined[span:, :] = dot3(
-        (gph[:, span:], gpl[:, span:]), (hth[...], htl[...]), 0, 0
-    )
-    gain_row = gain[...]
+
+    joined[span:, :] = (
+        dot3((gph[:, span:], gpl[:, span:]), (hth[...], htl[...]), 0, 0) * gain_row
+    )
     pieces, _, lanes = bc_part.shape
     across = width // lanes
-
-    def w_rows(lo, hi):
-        return wh[lo:hi, :].astype(F32) + wl[lo:hi, :].astype(F32)
-
-    gain_part = jnp.sum(joined[span:, :] * w_rows(span, pad), axis=0, keepdims=True)
     for row in range(pieces // across):
         for col in range(across):
-            lane = slice(col * lanes, (col + 1) * lanes)
-            block = joined[span + row * 8 : span + row * 8 + 8, lane] * gain_row[:, lane]
-            bc_part[row * across + col] = block
-    ba = []
-    for j in range(1, seqs):
-        to = lax.rem(seq + j, seqs)
-        ba.append(
-            remote(
-                bc_part.at[pl.ds(to * heads, heads)],
-                bc_seq.at[j - 1],
-                ba_s.at[j - 1],
-                ba_r.at[j - 1],
-                to,
-                head,
-            )
-        )
-        ba[-1].start()
-
-    @pl.loop(0, outs)
+            bc_part[row * across + col] = joined[
+                span + row * 8 : span + row * 8 + 8, col * lanes : (col + 1) * lanes
+            ]
+    mine = pl.ds(side * (pieces // 2), pieces // 2)
+    theirs = pl.ds((1 - side) * (pieces // 2), pieces // 2)
+    bc_core = remote(
+        bc_part.at[theirs], bc_half, a_sem.at[0], a_sem.at[1], partner, head
+    )
+    bc_core.start()
+    low = chans if chans % 128 == 0 else 0
+    rows = dot3((gph[:, low:span], gpl[:, low:span]), (hth[...], htl[...]), 0, 0)
+    joined[low:span, :] = rows * gain_row
+    inner = SeqSum(
+        joined, chans, keep, core_in, x_in, i_sems, inner_out, seq, head, seqs
+    )
+    inner.begin()
+    bc_core.wait()
+    bc_half[...] = bc_half[...] + bc_part[mine]
+
+    def others(make):
+        copies = []
+        for j in range(1, fars):
+            copies.append(make(j, lax.rem(far + j, fars)))
+            copies[-1].start()
+        return copies
+
+    cross_bc = others(
+        lambda j, to: remote(
+            bc_half.at[pl.ds(to * heads, heads)],
+            bc_seq.at[j - 1],
+            b_send.at[0, j - 1],
+            b_recv.at[0, j - 1],
+            2 * to + side,
+            head,
+        )
+    )
+    @pl.loop(1, reduce.outs)
     def _(step):
-        chunk_grad(step, at_in)
-
-    def weight_rows(n):
-        lo = n * chans
-        if chans % 128 == 0:
-            joined[lo : lo + chans, :] = dot3(
-                (gph[:, lo : lo + chans], gpl[:, lo : lo + chans]), (hth[...], htl[...]), 0, 0
-            )
-        elif n == 0:
-            joined[:span, :] = dot3((gph[:, :span], gpl[:, :span]), (hth[...], htl[...]), 0, 0)
-        part = jnp.sum(joined[lo : lo + chans, :] * w_rows(lo, lo + chans), 0, keepdims=True)
-        joined[lo : lo + chans, :] = joined[lo : lo + chans, :] * gain_row
-        keep[n] = joined[pl.ds(pl.multiple_of(lo + side * half, 8), half), :]
-        core[n] = remote(
-            joined.at[pl.ds(pl.multiple_of(lo + (1 - side) * half, 8), half)],
-            core_in.at[n],
-            c_send.at[n],
-            c_recv.at[n],
-            partner,
+        produce(step)
+
+    inner.pair()
+
+    small_mine[...] = small_in[...]
+
+    @pl.loop(0, heads)
+    def _(where):
+        rows = chunk_rows(where)
+        hat = hth[rows, :].astype(F32) + htl[rows, :].astype(F32)
+        small_mine[2, 0:1, :] = small_mine[2, 0:1, :] + jnp.sum(
+            parts[where] * hat, 0, keepdims=True
+        )
+
+    reduce.reduce(0)
+    small_mine[0] = joined[span + 2 * NSTATE : span + 2 * NSTATE + 8, :]
+    small_core = remote(
+        small_mine, small_pair, a_sem.at[2], a_sem.at[3], partner, head
+    )
+    small_core.start()
+    for copy in cross_bc:
+        copy.wait()
+    quarter = bc_half[pl.ds(far * heads, heads)]
+    for j in range(fars - 1):
+        quarter = quarter + bc_seq[j]
+    bc_quart[...] = quarter
+
+    def to_heads(make):
+        copies = []
+        for j in range(1, heads):
+            copies.append(make(j, lax.rem(head + j, heads)))
+            copies[-1].start()
+        return copies
+
+    spread_bc = to_heads(
+        lambda j, to: remote(
+            bc_quart.at[to], bc_head.at[j - 1], c_send.at[0, j - 1], c_recv.at[0, j - 1], seq, to
+        )
+    )
+    reduce.reduce(1)
+    small_core.wait()
+    small_far[far] = small_mine[...] + small_pair[...]
+    cross_small = others(
+        lambda j, to: remote(
+            small_far.at[far],
+            small_far.at[far],
+            m_sem.at[0, j - 1],
+            m_sem.at[1, j - 1],
+            2 * to + side,
             head,
         )
-        core[n].start()
-        return part
-
-    def z_copy(where, step, up):
-        goal = target(step)
-        return remote(
-            grads.at[where],
-            z_in.at[goal + (1 if up else 0)],
-            z_send.at[step],
-            z_recv.at[goal + (1 if up else 0)],
+    )
+    reduce.reduce(2)
+    reduce.reduce(3)
+    for copy in spread_bc:
+        copy.wait()
+    piece = bc_quart[head]
+    for j in range(heads - 1):
+        piece = piece + bc_head[j]
+    block = side * (pieces // 2) + far * heads
+    bc_full[block + head] = piece
+    gather_bc = to_heads(
+        lambda j, to: remote(
+            bc_full.at[block + head],
+            bc_full.at[block + head],
+            c_send.at[1, j - 1],
+            c_recv.at[1, j - 1],
             seq,
-            (at_out + (1 if up else -1)) * ins + at_in,
-        )
-
-    def z_wait(slot):
+            to,
+        )
+    )
+    for j in range(1, fars):
+        came = lax.rem(far - j + fars, fars)
         remote(
-            grads.at[0], z_in.at[slot], z_send.at[0], z_recv.at[slot], partner, head
+            small_far.at[came], small_far.at[came], m_sem.at[0, j - 1], m_sem.at[1, j - 1],
+            partner, head,
         ).wait_recv()
-
-    def reduce_step(step):
-        goal = target(step)
-        where = goal * ins + at_in
-        for j in range(ins - 1):
-            y_copy(step, j).wait_recv()
-            grads[where] = grads[where] + y_in[goal * (ins - 1) + j]
-        if step == outs - 1:
-
-            @pl.when(at_out > 0)
-            def _():
-                z_wait(goal + 1)
-                grads[where] = grads[where] + z_in[goal + 1]
-
-            @pl.when(at_out < outs - 1)
-            def _():
-                z_wait(goal)
-                grads[where] = grads[where] + z_in[goal]
-
-            return
-
-        @pl.when(goal > at_out)
-        def _():
-            @pl.when(at_out > 0)
-            def _():
-                z_wait(goal + 1)
-                grads[where] = grads[where] + z_in[goal + 1]
-
-            z_copy(where, step, True).start()
-
-        @pl.when(goal < at_out)
-        def _():
-            @pl.when(at_out < outs - 1)
-            def _():
-                z_wait(goal)
-                grads[where] = grads[where] + z_in[goal]
-
-            z_copy(where, step, False).start()
-
-    gain_part = gain_part + weight_rows(0)
-    reduce_step(0)
-    gain_part = gain_part + weight_rows(1)
-    after_core(0)
-
-    small_all[seq] = small_in[...]
-    small_all[seq, 0] = joined[span + 2 * NSTATE : span + 2 * NSTATE + 8, :] * gain_row
-    small_all[seq, 2, 0:1, :] = gain_part
-    sa = []
-    for j in range(1, seqs):
-        sa.append(
-            remote(
-                small_all.at[seq],
-                small_all.at[seq],
-                sa_s.at[j - 1],
-                sa_r.at[j - 1],
-                lax.rem(seq + j, seqs),
-                head,
-            )
-        )
-        sa[-1].start()
-    after_core(1)
-
-    for copy in ba:
-        copy.wait_recv()
-    own = pl.ds(seq * heads, heads)
-    bc_part[own] = bc_part[own] + bc_seq[0]
-    for j in range(1, seqs - 1):
-        bc_part[own] = bc_part[own] + bc_seq[j]
-    bb = []
-    for j in range(1, heads):
-        to = lax.rem(head + j, heads)
-        bb.append(
-            remote(
-                bc_part.at[seq * heads + to],
-                bc_head.at[j - 1],
-                bb_s.at[j - 1],
-                bb_r.at[j - 1],
-                seq,
-                to,
-            )
-        )
-        bb[-1].start()
-
-    def sent_from(j, count, at):
-        return lax.rem(at - j + count, count)
-
-    for j in range(1, seqs):
-        came = sent_from(j, seqs, seq)
-        remote(
-            small_all.at[came], small_all.at[came], sa_s.at[j - 1], sa_r.at[j - 1], partner, head
-        ).wait_recv()
-    total = small_all[0]
-    for j in range(1, seqs):
-        total = total + small_all[j]
+    total = small_far[0]
+    for j in range(1, fars):
+        total = total + small_far[j]
     small_out[...] = total
     small_head[head] = total[2]
-    sb = []
+    spread_small = to_heads(
+        lambda j, to: remote(
+            small_head.at[head], small_head.at[head], h_send.at[j - 1], h_recv.at[j - 1], seq, to
+        )
+    )
+    reduce.reduce(4)
+    reduce.reduce(5)
     for j in range(1, heads):
-        sb.append(
-            remote(
-                small_head.at[head],
-                small_head.at[head],
-                sb_s.at[j - 1],
-                sb_r.at[j - 1],
-                seq,
-                lax.rem(head + j, heads),
-            )
-        )
-        sb[-1].start()
-
-    reduce_step(1)
-    for copy in bb:
-        copy.wait_recv()
-    piece = bc_part[seq * heads + head]
-    for j in range(heads - 1):
-        piece = piece + bc_head[j]
-    here = seq * heads + head
-    bc_full[here] = piece
-    bc = []
+        came = lax.rem(head - j + heads, heads)
+        remote(
+            bc_full.at[block + came], bc_full.at[block + came],
+            c_send.at[1, j - 1], c_recv.at[1, j - 1], partner, head,
+        ).wait_recv()
+    reduce.reduce(6)
+    own_block = pl.ds(block, heads)
+    join_bc = others(
+        lambda j, to: remote(
+            bc_full.at[own_block],
+            bc_full.at[own_block],
+            b_send.at[1, j - 1],
+            b_recv.at[1, j - 1],
+            2 * to + side,
+            head,
+        )
+    )
     for j in range(1, heads):
-        bc.append(
-            remote(
-                bc_full.at[here],
-                bc_full.at[here],
-                bc_s.at[j - 1],
-                bc_r.at[j - 1],
-                seq,
-                lax.rem(head + j, heads),
-            )
-        )
-        bc[-1].start()
-    for j in range(1, heads):
-        came = sent_from(j, heads, head)
+        came = lax.rem(head - j + heads, heads)
         remote(
-            small_head.at[came], small_head.at[came], sb_s.at[j - 1], sb_r.at[j - 1], seq, came
+            small_head.at[came], small_head.at[came], h_send.at[j - 1], h_recv.at[j - 1], seq, came
         ).wait_recv()
     total = small_head[0]
     for j in range(1, heads):
         total = total + small_head[j]
     small_out[2] = total
-    for j in range(1, heads):
-        came = seq * heads + sent_from(j, heads, head)
+    for j in range(1, fars):
+        came = side * (pieces // 2) + lax.rem(far - j + fars, fars) * heads
+        came = pl.ds(came, heads)
         remote(
-            bc_full.at[came], bc_full.at[came], bc_s.at[j - 1], bc_r.at[j - 1], partner, head
+            bc_full.at[came], bc_full.at[came], b_send.at[1, j - 1], b_recv.at[1, j - 1],
+            partner, head,
         ).wait_recv()
-    bd = []
-    for j in range(1, seqs):
-        bd.append(
-            remote(
-                bc_full.at[own],
-                bc_full.at[own],
-                bd_s.at[j - 1],
-                bd_r.at[j - 1],
-                lax.rem(seq + j, seqs),
-                head,
-            )
-        )
-        bd[-1].start()
-    for step in range(2, outs - 1):
-        reduce_step(step)
-    after_x(0, gate_out)
-    reduce_step(outs - 1)
-    where = at_out * ins + at_in
-    grad_hat = grads[where] * gain_row
-    rows = resid[...]
-    scale = lax.rsqrt(jnp.mean(rows * rows, axis=1, keepdims=True) + EPSILON)
-    row_cross = jnp.sum(grad_hat * rows, axis=1, keepdims=True)
+    join_core = remote(
+        bc_full.at[mine], bc_full.at[mine], a_sem.at[4], a_sem.at[5], partner, head
+    )
+    join_core.start()
+    inner.total()
+    reduce.reduce(7)
+    reduce.last()
+    grad_hat = parts[head] * gain_row
+    values = resid[...]
+    scale = lax.rsqrt(jnp.mean(values * values, axis=1, keepdims=True) + EPSILON)
+    row_cross = jnp.sum(grad_hat * values, axis=1, keepdims=True)
     resid_grad[...] = (
-        cot[...] + scale * grad_hat - rows * (scale * scale * scale * (row_cross / width))
-    )
-    after_x(1, inner_out)
-    for j in range(1, seqs):
-        came = pl.ds(sent_from(j, seqs, seq) * heads, heads)
-        remote(
-            bc_full.at[came], bc_full.at[came], bd_s.at[j - 1], bd_r.at[j - 1], partner, head
-        ).wait_recv()
-    bc_put = pltpu.make_async_copy(bc_full, bc_out, o_sem.at[2])
+        cot[...] + scale * grad_hat - values * (scale * scale * scale * (row_cross / width))
+    )
+    remote(
+        bc_full.at[theirs], bc_full.at[theirs], a_sem.at[4], a_sem.at[5], partner, head
+    ).wait_recv()
+    bc_put = pltpu.make_async_copy(bc_full, bc_out, put_sem)
     bc_put.start()
-
-    @pl.loop(0, outs)
-    def _(step):
-        for j in range(ins - 1):
-            y_copy(step, j).wait_send()
-
-    for step in range(outs - 1):
-        remote(
-            grads.at[0], z_in.at[0], z_send.at[step], z_recv.at[0], partner, head
-        ).wait_send()
-    for copy in ba + bb + bc + bd + sa + sb:
+    reduce.finish()
+    for copy in gather_bc + cross_small + spread_small + join_bc + [join_core]:
         copy.wait_send()
-    for n in range(2):
-        finals[n].wait_send()
-        remote(
-            keep.at[n],
-            (gate_out, inner_out)[n].at[theirs],
-            f_send.at[n],
-            f_recv.at[n],
-            partner,
-            head,
-        ).wait_recv()
-        puts[n].wait()
+    inner.end()
     bc_put.wait()
 
 
@@ -443,24 +389,22 @@
     ins = inner_count(heads)
     outs = heads // ins
     rounds = (seqs // 2).bit_length() - 1
-    half = chans // 2
+    fars = seqs // 2
     lanes = 2 * NSTATE * width // (8 * seqs * heads)
     pieces = seqs * heads
     anywhere = pl.BlockSpec(memory_space=pl.ANY)
     local = pl.BlockSpec(memory_space=pltpu.VMEM)
     sems = pltpu.SemaphoreType.DMA
-    weight_shape = jax.ShapeDtypeStruct((chans, width), F32)
     return pl.pallas_call(
         functools.partial(tail_kernel, (seqs, heads, chunk, chans, pad)),
         out_shape=(
             jax.ShapeDtypeStruct((chunk, width), F32),
-            weight_shape,
-            weight_shape,
+            jax.ShapeDtypeStruct((chans, width), F32),
             jax.ShapeDtypeStruct((pieces, 8, lanes), F32),
             jax.ShapeDtypeStruct((3, 8, width), F32),
         ),
         in_specs=[anywhere] * 6 + [local] * 4,
-        out_specs=(local, anywhere, anywhere, anywhere, local),
+        out_specs=(local, anywhere, anywhere, local),
         scratch_shapes=[
             pltpu.VMEM((tokens, pad), BF16),
             pltpu.VMEM((tokens, pad), BF16),
@@ -472,39 +416,28 @@
             pltpu.VMEM((outs * (ins - 1), chunk, width), F32),
             pltpu.VMEM((outs + 1, chunk, width), F32),
             pltpu.VMEM((pad, width), F32),
-            pltpu.VMEM((2, half, width), F32),
-            pltpu.VMEM((2, half, width), F32),
-            pltpu.VMEM((2, rounds, half, width), F32),
+            *seq_sum_scratch(chans // 2, width, rounds),
             pltpu.VMEM((pieces, 8, lanes), F32),
-            pltpu.VMEM((seqs - 1, heads, 8, lanes), F32),
+            pltpu.VMEM((pieces // 2, 8, lanes), F32),
+            pltpu.VMEM((fars - 1, heads, 8, lanes), F32),
+            pltpu.VMEM((heads, 8, lanes), F32),
             pltpu.VMEM((heads - 1, 8, lanes), F32),
             pltpu.VMEM((pieces, 8, lanes), F32),
-            pltpu.VMEM((seqs, 3, 8, width), F32),
+            pltpu.VMEM((3, 8, width), F32),
+            pltpu.VMEM((3, 8, width), F32),
+            pltpu.VMEM((fars, 3, 8, width), F32),
             pltpu.VMEM((heads, 8, width), F32),
             sems((6,)),
-            sems((outs * (ins - 1),)),
-            sems((outs * (ins - 1),)),
-            sems((outs,)),
-            sems((outs + 1,)),
-            sems((2,)),
-            sems((2,)),
-            sems((2, rounds)),
-            sems((2, rounds)),
-            sems((2,)),
-            sems((2,)),
-            sems((3,)),
-            sems((seqs - 1,)),
-            sems((seqs - 1,)),
+            *line_reduce_sems(ins, outs),
+            sems((6,)),
+            sems((2, fars - 1)),
+            sems((2, fars - 1)),
+            sems((2, heads - 1)),
+            sems((2, heads - 1)),
+            sems((2, fars - 1)),
             sems((heads - 1,)),
             sems((heads - 1,)),
-            sems((heads - 1,)),
-            sems((heads - 1,)),
-            sems((seqs - 1,)),
-            sems((seqs - 1,)),
-            sems((seqs - 1,)),
-            sems((seqs - 1,)),
-            sems((heads - 1,)),
-            sems((heads - 1,)),
+            sems,
         ],
         compiler_params=pltpu.CompilerParams(
             collective_id=1, has_side_effects=True, vmem_limit_bytes=VMEM_LIMIT
@@ -835,6 +768,22 @@
     return [(lo, min(lo + 2 * HEADDIM, chans)) for lo in range(0, chans, 2 * HEADDIM)]
 
 
+def spread(values, expand):
+    top, low = halves(values)
+    expand = expand.astype(BF16)
+    dims = (((1,), (0,)), ((), ()))
+    one = functools.partial(lax.dot_general, dimension_numbers=dims, preferred_element_type=F32)
+    return one(top, expand) + one(low, expand)
+
+
+def gather_heads(values, expand):
+    top, low = halves(values)
+    expand = expand.astype(BF16)
+    dims = (((1,), (1,)), ((), ()))
+    one = functools.partial(lax.dot_general, dimension_numbers=dims, preferred_element_type=F32)
+    return one(top, expand) + one(low, expand)
+
+
 def row_scale(total_row, expand):
     wide = jnp.broadcast_to(jnp.exp(total_row), (128, 128)).T
     return dotx(expand, wide, 0, 0)
@@ -853,8 +802,8 @@
     seqs, heads, chunk, chans, pad = dims
     (
         proj, cot, out_w, conv_p, head_p, chan_p, expand_in,
-        cot_hi, cot_lo, conv_o, cum_o, step_o, state_o, mixed_o, cross_o, stat_o, edge_o,
-        parts, hi, lo, pj, raw, owh, owl, scaled, enter, prefix, run, exch, stat_all, lows,
+        cot_hi, cot_lo, conv_hbm, cum_o, step_o, state_o, mixed_o, cross_o, stat_o, edge_o,
+        parts, hi, lo, pj, conv_o, raw, owh, owl, scaled, enter, prefix, run, exch, stat_all, lows,
         z_send, z_recv, y_send, y_recv, load_sem, put_sem, e_send, e_recv,
         s_send, s_recv, t_send, t_recv,
     ) = refs
@@ -913,16 +862,18 @@
         last = cum[BLOCK - 1 : BLOCK, :]
         step_o[here, :] = step
         cum_o[here, :] = cum
-        fed = act[:, :chans] * dotx(step, expand, 1, 0)
+        fed = act[:, :chans] * spread(step, expand)
         scaled[here, :] = fed
         fresh = dotx(
-            fed * dotx(jnp.exp(last - cum), expand, 1, 0), act[:, chans : chans + NSTATE], 0, 0
+            fed * spread(jnp.exp(last - cum), expand), act[:, chans : chans + NSTATE], 0, 0
         )
         enter[b] = run[...]
         run[...] = row_scale(last, expand) * run[...] + fresh
         prefix[pl.ds(b + 1, 1), :] = prefix[pl.ds(b, 1), :] + last
 
     gather.relay(1)
+    conv_put = pltpu.make_async_copy(conv_o, conv_hbm, put_sem.at[2 * heads])
+    conv_put.start()
     exch[seq, 0:chans, :] = run[...]
     exch[seq, chans : chans + 8, :] = jnp.broadcast_to(prefix[blocks : blocks + 1, :], (8, 128))
 
@@ -986,7 +937,7 @@
         carried = dotx(act[:, chans + NSTATE :], state, 1, 1)
         mixed = (
             mixed_o[here, :]
-            + carried * dotx(jnp.exp(cum_o[here, :]), expand, 1, 0)
+            + carried * spread(jnp.exp(cum_o[here, :]), expand)
             + chan_p[1:2, :] * act[:, :chans]
         )
         mixed_o[here, :] = mixed
@@ -1038,6 +989,7 @@
         )
         sends[-1].start()
     gather.finish()
+    conv_put.wait()
 
     @pl.loop(0, heads)
     def _(where):
@@ -1091,12 +1043,13 @@
             shape((8, pad), F32),
         ),
         in_specs=[anywhere, local, anywhere, local, local, local, local],
-        out_specs=(anywhere, anywhere) + (local,) * 8,
+        out_specs=(anywhere, anywhere, anywhere) + (local,) * 7,
         scratch_shapes=[
             pltpu.VMEM((heads, chunk, width), F32),
             pltpu.VMEM((heads, chunk, width), BF16),
             pltpu.VMEM((heads, chunk, width), BF16),
             pltpu.VMEM((8 + tokens, pad), F32),
+            pltpu.VMEM((tokens, wide), F32),
             pltpu.VMEM((chans, width), F32),
             pltpu.VMEM((width, chans), BF16),
             pltpu.VMEM((width, chans), BF16),
@@ -1112,7 +1065,7 @@
             sems((outs, ins - 1)),
             sems((outs, ins - 1)),
             sems((2,)),
-            sems((2 * heads,)),
+            sems((2 * heads + 1,)),
             sems,
             sems,
             sems((seqs - 1,)),
@@ -1134,6 +1087,8 @@
         self.seq, self.partner = seq, partner
         self.ins = inner_count(heads)
         self.outs = heads // self.ins
+        self.half = parts.shape[1] // 2
+        self.turns = 2 * self.outs
         self.at_out, self.at_in = head // self.ins, lax.rem(head, self.ins)
         self.upper = self.at_out // (self.outs // 2)
         self.mirrored = self.at_out + self.upper * (self.outs - 1 - 2 * self.at_out)
@@ -1145,112 +1100,148 @@
         far = far + self.upper * (self.outs - 1 - 2 * far)
         return far + last * (self.at_out - far)
 
-    def y_copy(self, step, j):
+    def rows(self, turn):
+        return pl.ds(pl.multiple_of(lax.rem(turn, 2) * self.half, 8), self.half)
+
+    def y_copy(self, turn, j):
+        goal = self.target(turn // 2)
         to = lax.rem(self.at_in + 1 + j, self.ins)
-        slot = self.target(step) * (self.ins - 1) + j
+        rows = self.rows(turn)
         return remote(
-            self.parts.at[self.target(step) * self.ins + to],
-            self.y_in.at[slot],
-            self.y_send.at[slot],
-            self.y_recv.at[slot],
+            self.parts.at[goal * self.ins + to, rows],
+            self.y_in.at[goal * (self.ins - 1) + j, rows],
+            self.y_send.at[turn, j],
+            self.y_recv.at[turn, j],
             self.seq,
             self.at_out * self.ins + to,
         )
 
-    def give(self, make):
-        @pl.loop(0, self.outs)
-        def _(step):
-            for j in range(self.ins - 1):
-                make(self.target(step) * self.ins + lax.rem(self.at_in + 1 + j, self.ins))
-                self.y_copy(step, j).start()
-
-    def own(self, make):
-        @pl.loop(0, self.outs)
-        def _(step):
-            make(self.target(step) * self.ins + self.at_in)
-
-    def take(self, where, slot):
+    def give(self, turn):
+        for j in range(self.ins - 1):
+            self.y_copy(turn, j).start()
+
+    def take(self, turn, slot):
+        rows = self.rows(turn)
+        where = self.target(turn // 2) * self.ins + self.at_in
         remote(
-            self.parts.at[0],
-            self.z_in.at[slot],
+            self.parts.at[0, rows],
+            self.z_in.at[slot, rows],
             self.z_send.at[0],
-            self.z_recv.at[slot],
+            self.z_recv.at[slot, lax.rem(turn, 2)],
             self.partner,
             self.at_out * self.ins + self.at_in,
         ).wait_recv()
-        self.parts[where] = self.parts[where] + self.z_in[slot]
-
-    def pass_on(self, where, step, up):
-        slot = self.target(step) + up
+        self.parts[where, rows, :] = self.parts[where, rows, :] + self.z_in[slot, rows, :]
+
+    def pass_on(self, turn, up):
+        goal, rows = self.target(turn // 2), self.rows(turn)
         remote(
-            self.parts.at[where],
-            self.z_in.at[slot],
-            self.z_send.at[step],
-            self.z_recv.at[slot],
+            self.parts.at[goal * self.ins + self.at_in, rows],
+            self.z_in.at[goal + up, rows],
+            self.z_send.at[turn],
+            self.z_recv.at[goal + up, lax.rem(turn, 2)],
             self.seq,
             (self.at_out + 2 * up - 1) * self.ins + self.at_in,
         ).start()
 
-    def reduce(self, step):
-        goal = self.target(step)
+    def across(self, turn):
+        goal = self.target(turn // 2)
+        rows = self.rows(turn)
         where = goal * self.ins + self.at_in
         for j in range(self.ins - 1):
-            self.y_copy(step, j).wait_recv()
-            self.parts[where] = self.parts[where] + self.y_in[goal * (self.ins - 1) + j]
-        from_below, from_above = self.at_out > 0, self.at_out < self.outs - 1
-
-        @pl.when((goal >= self.at_out) & from_below)
-        def _():
-            self.take(where, goal + 1)
-
-        @pl.when((goal <= self.at_out) & from_above)
-        def _():
-            self.take(where, goal)
-
-        if step < self.outs - 1:
-
-            @pl.when(goal > self.at_out)
-            def _():
-                self.pass_on(where, step, 1)
-
-            @pl.when(goal < self.at_out)
-            def _():
-                self.pass_on(where, step, 0)
+            self.y_copy(turn, j).wait_recv()
+
+        @pl.when(turn + 2 < self.turns)
+        def _():
+            self.give(turn + 2)
+
+        for j in range(self.ins - 1):
+            self.parts[where, rows, :] = (
+                self.parts[where, rows, :] + self.y_in[goal * (self.ins - 1) + j, rows, :]
+            )
+
+        @pl.when((goal > self.at_out) & (self.at_out == 0))
+        def _():
+            self.pass_on(turn, 1)
+
+        @pl.when((goal < self.at_out) & (self.at_out == self.outs - 1))
+        def _():
+            self.pass_on(turn, 0)
+
+    def along(self, turn):
+        goal = self.target(turn // 2)
+
+        @pl.when((goal >= self.at_out) & (self.at_out > 0))
+        def _():
+            self.take(turn, goal + 1)
+
+        @pl.when((goal <= self.at_out) & (self.at_out < self.outs - 1))
+        def _():
+            self.take(turn, goal)
+
+        @pl.when((goal > self.at_out) & (self.at_out > 0))
+        def _():
+            self.pass_on(turn, 1)
+
+        @pl.when((goal < self.at_out) & (self.at_out < self.outs - 1))
+        def _():
+            self.pass_on(turn, 0)
+
+    def reduce(self, turn):
+        turn = jnp.int32(turn)
+        self.across(turn)
+
+        @pl.when(turn > 0)
+        def _():
+            self.along(turn - 1)
+
+    def last(self):
+        self.along(jnp.int32(self.turns - 1))
 
     def finish(self):
-        @pl.loop(0, self.outs)
-        def _(step):
+        @pl.loop(0, self.turns)
+        def _(turn):
             for j in range(self.ins - 1):
-                self.y_copy(step, j).wait_send()
-
-        for step in range(self.outs - 1):
+                self.y_copy(turn, j).wait_send()
+
+        @pl.loop(0, self.turns - 2)
+        def _(turn):
+            rows = pl.ds(0, self.half)
             remote(
-                self.parts.at[0],
-                self.z_in.at[0],
-                self.z_send.at[step],
-                self.z_recv.at[0],
+                self.parts.at[0, rows],
+                self.z_in.at[0, rows],
+                self.z_send.at[turn],
+                self.z_recv.at[0, 0],
                 self.partner,
                 self.at_out * self.ins + self.at_in,
             ).wait_send()
 
 
+def line_reduce_sems(ins, outs):
+    sems = pltpu.SemaphoreType.DMA
+    return [
+        sems((2 * outs, ins - 1)),
+        sems((2 * outs, ins - 1)),
+        sems((2 * outs,)),
+        sems((outs + 1, 2)),
+    ]
+
+
 def backward_kernel(dims, *refs):
     seqs, heads, chunk, chans, pad = dims
     (
-        proj, edge_in, cot_hi, cot_lo, conv_in, cum_in, step_in, state_in, mixed_in, cross_in,
-        stat_in, out_w, resid, conv_p, head_p, chan_p, expand_in,
-        result_o, gp_hi, gp_lo, out_o, wide_o, chan_o, head_o,
+        proj, edge_in, cot_hi, cot_lo, hat_hi, hat_lo, conv_in, cum_in, step_in, state_in, mixed_in, cross_in,
+        stat_in, out_w, resid, conv_p, head_p, chan_p, gain, expand_in,
+        result_o, gp_hi, gp_lo, out_o, gate_o, wide_o, chan_o, head_o,
         pj, ngh, ngl, owh, owl, gmix, fedg, adj, run, exch, gconv,
-        parts, y_in, z_in, chi, clo, oparts, keep, core_in, x_in, head_acc,
-        y_send, y_recv, z_send, z_recv, load_sem, s_send, s_recv, e_send, e_recv,
-        c_send, c_recv, x_send, x_recv, f_send, f_recv, o_sem,
+        parts, y_in, z_in, chi, clo, oparts, columns, conv_buf, head_acc,
+        keep_o, core_o, x_o, o_sems, keep_g, core_g, x_g, g_sems,
+        y_send, y_recv, z_send, z_recv, load_sem, s_send, s_recv, e_send, e_recv, conv_sem,
     ) = refs
     tokens = chunk * heads
     blocks = tokens // BLOCK
     span = 2 * chans
     wide = chans + 2 * NSTATE
-    half = chans // 2
-    rounds = (seqs // 2).bit_length() - 1
     split_at = resid.shape[1] // 2
     seq, head = lax.axis_index("seq"), lax.axis_index("head")
     side = lax.rem(seq, 2)
@@ -1283,51 +1274,129 @@
     run[...] = jnp.zeros_like(run)
     for load in loads[:2]:
         load.wait()
-    per = BLOCK // 128
     groups = tokens // 128
     turned_stats = stat_in[...].T
-    inner_total = DI_TOTAL(heads, chans)
+    inner_total = float(heads * chans)
     gain_row, skip_row = chan_p[0:1, :], chan_p[1:2, :]
-
-    for b in range(blocks - 1, -1, -1):
-        at = b * BLOCK
-        here = slice(at, at + BLOCK)
-        squares = jnp.concatenate(
-            [turned_stats[:, b * per + n : b * per + n + 1] for n in range(per)], 0
-        )
-        cross = jnp.concatenate(
-            [
-                turned_stats[:, groups + b * per + n : groups + b * per + n + 1]
-                for n in range(per)
-            ],
-            0,
-        )
-        scale = lax.rsqrt(squares / inner_total + EPSILON)
-        factor = scale * scale * scale * (cross / inner_total)
-        gate = pj[at + 8 : at + 8 + BLOCK, 0:chans]
+    for n in range(groups):
+        here = slice(n * 128, n * 128 + 128)
+        scale = lax.rsqrt(turned_stats[:, n : n + 1] / inner_total + EPSILON)
+        cross = turned_stats[:, groups + n : groups + n + 1]
+        columns[here, 0:1] = scale
+        columns[here, 1:2] = scale * scale * scale * (cross / inner_total)
+
+    def conv_load(b, slot):
+        return pltpu.make_async_copy(
+            conv_in.at[pl.ds(pl.multiple_of(b * BLOCK, BLOCK), BLOCK)],
+            conv_buf.at[slot],
+            conv_sem.at[slot],
+        )
+
+    def conv_of(n, b, following):
+        slot = lax.rem(n, 2)
+        conv_load(b, slot).wait()
+        conv_load(following, 1 - slot).start()
+        return conv_buf[slot]
+
+    conv_load(blocks - 1, 0).start()
+
+    @pl.loop(0, blocks)
+    def _(b):
+        at = pl.multiple_of(b * BLOCK, BLOCK)
+        here = pl.ds(at, BLOCK)
+        gate = pj[pl.ds(at + 8, BLOCK), 0:chans]
+        ngh[here, :], ngl[here, :] = halves(
+            mixed_in[here, :] * (gate * logistic(gate)) * columns[here, 0:1] * gain_row
+        )
+
+    reduce = LineReduce(
+        parts, y_in, z_in, (y_send, y_recv, z_send, z_recv), seq, head, heads, partner
+    )
+
+    ins = reduce.ins
+
+    def produce(step):
+        first = reduce.target(step) * ins
+        rows = pl.ds(pl.multiple_of(first * chunk, 8), ins * chunk)
+        out = dot3((ngh[rows, :], ngl[rows, :]), (owh[...], owl[...]), 1, 0)
+        for n in range(ins):
+            parts[first + n] = out[n * chunk : (n + 1) * chunk]
+
+    @pl.loop(0, reduce.outs)
+    def _(step):
+        produce(step)
+
+        @pl.when(step == 0)
+        def _():
+            reduce.give(jnp.int32(0))
+            reduce.give(jnp.int32(1))
+
+    for load in loads[2:4]:
+        load.wait()
+
+    def weight_parts(left_hi, left_lo, hi, lo, then):
+        for n in range(2):
+            cols = pl.ds(n * split_at, split_at)
+            oparts[:, n * split_at : (n + 1) * split_at] = dot3(
+                (left_hi[...], left_lo[...]), (chi[...], clo[...]), 0, 0
+            )
+            source, cols = ((hi, lo), pl.ds(split_at, split_at)) if n == 0 else (then, None)
+            if source is None:
+                continue
+            cols = pl.ds(split_at, split_at) if n == 0 else pl.ds(0, split_at)
+            more = [
+                pltpu.make_async_copy(a.at[:, cols], b, load_sem.at[2 + m])
+                for m, (a, b) in enumerate(zip(source, (chi, clo)))
+            ]
+            for load in more:
+                load.start()
+            if n == 0:
+                for load in more:
+                    load.wait()
+        return more
+
+    hat_load = weight_parts(ngh, ngl, cot_hi, cot_lo, (hat_hi, hat_lo))
+    out_sum = SeqSum(oparts, 0, keep_o, core_o, x_o, o_sems, out_o, seq, head, seqs)
+    out_sum.begin()
+    reduce.reduce(0)
+    out_sum.pair()
+
+    def poll(n, base):
+        @pl.when(lax.rem(n, pace) == pace - 1)
+        def _():
+            reduce.reduce(base + n // pace)
+
+    pace = max(1, blocks // 2)
+
+    @pl.loop(0, blocks)
+    def _(back):
+        b = blocks - 1 - back
+        at = pl.multiple_of(b * BLOCK, BLOCK)
+        here = pl.ds(at, BLOCK)
+        scale = columns[here, 0:1]
+        gate = pj[pl.ds(at + 8, BLOCK), 0:chans]
         sig = logistic(gate)
         gate_act = gate * sig
         mixed = mixed_in[here, :]
         gated = mixed * gate_act
         grad_ng = cross_in[here, :]
-        grad_gated = scale * (grad_ng * gain_row) - gated * factor
-        scaled = gated * scale
-        ngh[here, :], ngl[here, :] = halves(scaled * gain_row)
+        grad_gated = scale * (grad_ng * gain_row) - gated * columns[here, 1:2]
         grad_mixed = grad_gated * gate_act
         gmix[here, :] = grad_mixed
         gp_hi[here, 0:chans], gp_lo[here, 0:chans] = halves(
             grad_gated * mixed * (sig * (1.0 + gate * (1.0 - sig)))
         )
-        conv = conv_in[here, :]
+        conv = conv_of(back, b, jnp.maximum(b - 1, 0))
         act = conv * logistic(conv)
-        chan_o[0:1, :] = chan_o[0:1, :] + jnp.sum(grad_ng * scaled, 0, keepdims=True)
+        chan_o[0:1, :] = chan_o[0:1, :] + jnp.sum(grad_ng * (gated * scale), 0, keepdims=True)
         chan_o[1:2, :] = chan_o[1:2, :] + jnp.sum(grad_mixed * act[:, :chans], 0, keepdims=True)
-        early = grad_mixed * dotx(jnp.exp(cum_in[here, :]), expand, 1, 0)
+        early = grad_mixed * spread(jnp.exp(cum_in[here, :]), expand)
         adj[b] = run[...]
-        run[...] = row_scale(cum_in[at + BLOCK - 1 : at + BLOCK, :], expand) * run[...] + dotx(
+        run[...] = row_scale(cum_in[pl.ds(at + BLOCK - 1, 1), :], expand) * run[...] + dotx(
             early, act[:, chans + NSTATE :], 0, 0
         )
         gconv[here, chans + NSTATE :] = dotx(early, state_in[b], 1, 0)
+        poll(back, 1)
 
     total = jnp.zeros((1, 128), F32)
     for b in range(blocks):
@@ -1344,76 +1413,46 @@
         def _():
             state_copy(seq, j, seq - j).start()
 
-    reduce = LineReduce(
-        parts, y_in, z_in, (y_send, y_recv, z_send, z_recv), seq, head, heads, partner
-    )
-
-    def product_chunk(where):
-        rows = pl.ds(pl.multiple_of(where * chunk, 8), chunk)
-        parts[where] = dot3((ngh[rows, :], ngl[rows, :]), (owh[...], owl[...]), 1, 0)
-
-    reduce.give(product_chunk)
-    for load in loads[2:4]:
+    for load in hat_load:
         load.wait()
-    oparts[:, :split_at] = dot3((ngh[...], ngl[...]), (chi[...], clo[...]), 0, 0)
-    rest = [
-        pltpu.make_async_copy(a.at[:, pl.ds(split_at, split_at)], b, load_sem.at[n])
-        for n, (a, b) in enumerate(((cot_hi, chi), (cot_lo, clo)))
-    ]
-    for load in rest:
-        load.start()
-    reduce.own(product_chunk)
-    for load in rest:
-        load.wait()
-    oparts[:, split_at:] = dot3((ngh[...], ngl[...]), (chi[...], clo[...]), 0, 0)
-    mine = pl.ds(pl.multiple_of(side * half, 8), half)
-    theirs = pl.ds(pl.multiple_of((1 - side) * half, 8), half)
-    keep[...] = oparts[mine, :]
-    core = remote(oparts.at[theirs], core_in, c_send, c_recv, partner, head)
-    core.start()
+    weight_parts(gp_hi.at[:, 0:chans], gp_lo.at[:, 0:chans], hat_hi, hat_lo, None)
+    oparts[...] = oparts[...] * gain[...]
+    gate_sum = SeqSum(oparts, 0, keep_g, core_g, x_g, g_sems, gate_o, seq, head, seqs)
+    gate_sum.begin()
+    reduce.reduce(3)
 
     @pl.loop(0, blocks)
     def _(b):
         at = pl.multiple_of(b * BLOCK, BLOCK)
         here = pl.ds(at, BLOCK)
-        conv = conv_in[here, :]
+        conv = conv_of(b, b, lax.rem(b + 1, blocks))
         act = conv * logistic(conv)
         writes, reads = act[:, chans : chans + NSTATE], act[:, chans + NSTATE :]
         scores = dotx(reads, writes, 1, 1)
         cum = cum_in[here, :]
         turned = cum.T
-        fed_all = act[:, :chans] * dotx(step_in[here, :], expand, 1, 0)
+        fed_all = act[:, :chans] * spread(step_in[here, :], expand)
         grad_scores = jnp.zeros((BLOCK, BLOCK), F32)
         for first_lane, end in lanes_of(chans):
             fed = fed_all[:, first_lane:end]
             grad = gmix[here, first_lane:end]
+            fed_parts, grad_parts = halves(fed), halves(grad)
             lane = lax.broadcasted_iota(jnp.int32, fed.shape, 1)
             outs = []
             for start in range(first_lane, end, HEADDIM):
                 decay = decay_of(cum, turned, start // HEADDIM, causal)
                 inside = (lane // HEADDIM) == (start - first_lane) // HEADDIM
-                grad_scores = grad_scores + decay * dotx(jnp.where(inside, grad, 0.0), fed, 1, 1)
-                outs.append(dotx(decay * scores, grad, 0, 0))
+                grad_scores = grad_scores + decay * dot3(halves(jnp.where(inside, grad, 0.0)), fed_parts, 1, 1)
+                outs.append(dot3(halves(decay * scores), grad_parts, 0, 0))
             out = outs[0]
             if len(outs) == 2:
                 out = jnp.where(lane < HEADDIM, outs[0], outs[1])
             fedg[here, first_lane:end] = out
         gconv[here, chans : chans + NSTATE] = dotx(grad_scores, reads, 0, 0)
         gconv[here, chans + NSTATE :] = gconv[here, chans + NSTATE :] + dotx(grad_scores, writes, 1, 0)
-
-    core.wait()
-    keep[...] = keep[...] + core_in[...]
-    x_copies = []
-
-    def x_start(source, turn):
-        far = seq + (2 << turn) - 2 * (2 << turn) * lax.rem(seq // (2 << turn), 2)
-        x_copies.append(
-            remote(source, x_in.at[turn], x_send.at[turn], x_recv.at[turn], far, head)
-        )
-        x_copies[-1].start()
-
-    x_start(keep, 0)
-    reduce.reduce(0)
+        poll(b, 4)
+
+    gate_sum.pair()
     run[...] = jnp.zeros_like(run)
     for back in range(seqs - 1):
         later = seqs - 1 - back
@@ -1441,7 +1480,7 @@
     def _(b):
         at = pl.multiple_of(b * BLOCK, BLOCK)
         here = pl.ds(at, BLOCK)
-        conv = conv_in[here, :]
+        conv = conv_of(b, b, lax.rem(b + 1, blocks))
         sig = logistic(conv)
         act = conv * sig
         slope = sig * (1.0 + conv * (1.0 - sig))
@@ -1449,20 +1488,20 @@
         cum = cum_in[here, :]
         step = step_in[here, :]
         last = cum[BLOCK - 1 : BLOCK, :]
-        step_wide = dotx(step, expand, 1, 0)
-        tails = dotx(jnp.exp(last - cum), expand, 1, 0)
+        step_wide = spread(step, expand)
+        tails = spread(jnp.exp(last - cum), expand)
         fed = inner * step_wide
         grad_state = adj[b]
         from_state = tails * dotx(writes, grad_state, 1, 1)
         grad_fed = fedg[here, :] + from_state
         grad_mixed = gmix[here, :]
         grad_writes = gconv[here, chans : chans + NSTATE] + dotx(fed * tails, grad_state, 1, 0)
-        direct = dotx(inner * grad_fed, expand, 1, 1)
+        direct = gather_heads(inner * grad_fed, expand)
         scanned = mixed_in[here, :] - skip_row * inner
         grad_cum = dotx(grad_mixed * scanned - fed * grad_fed, expand, 1, 1)
         kept = dotx(expand, grad_state * state_in[b], 1, 0)
         kept = dotx(lane_ones, kept, 1, 1)[0:1, :] * jnp.exp(last)
-        grad_last = kept + jnp.sum(dotx(fed * from_state, expand, 1, 1), 0, keepdims=True)
+        grad_last = kept + jnp.sum(gather_heads(fed * from_state, expand), 0, keepdims=True)
         grad_log = dotx(upper, grad_cum, 1, 0) + grad_last
         rate = head_p[1:2, :]
         head_acc[1:2, :] = head_acc[1:2, :] + jnp.sum(step * grad_log, 0, keepdims=True) * rate
@@ -1476,7 +1515,8 @@
         gconv[here, chans : chans + NSTATE] = grad_writes * slope[:, chans : chans + NSTATE]
         gconv[here, chans + NSTATE :] = gconv[here, chans + NSTATE :] * slope[:, chans + NSTATE :]
 
-    reduce.reduce(1)
+    out_sum.total()
+    reduce.reduce(6)
     edge = remote(
         gconv.at[pl.ds(0, 8)],
         gconv.at[pl.ds(tokens, 8)],
@@ -1517,21 +1557,11 @@
     def _(b):
         conv_back(b)
 
-    for step in range(2, reduce.outs - 1):
-        reduce.reduce(step)
-    now, new = keep, core_in
-    for turn in range(rounds):
-        x_copies[turn].wait()
-        new[...] = now[...] + x_in[turn]
-        now, new = new, now
-        if turn + 1 < rounds:
-            x_start(now, turn + 1)
-    put = pltpu.make_async_copy(now, out_o.at[mine], o_sem)
-    put.start()
-    final = remote(now, out_o.at[mine], f_send, f_recv, partner, head)
-    final.start()
-    reduce.reduce(reduce.outs - 1)
+    gate_sum.total()
+    reduce.reduce(7)
+    reduce.last()
     result_o[...] = resid[...] + parts[head]
+    conv_load(0, 0).wait()
     reduce.finish()
     for j in range(1, seqs):
 
@@ -1539,16 +1569,11 @@
         def _():
             state_copy(seq, j, seq - j).wait_send()
 
-    final.wait_send()
-    remote(now, out_o.at[theirs], f_send, f_recv, partner, head).wait_recv()
-    put.wait()
-
-
-def DI_TOTAL(heads, chans):
-    return float(heads * chans)
-
-
-def backward(proj, kept, out_w, resid, conv_p, head_p, chan_p, expand, seqs, heads):
+    out_sum.end()
+    gate_sum.end()
+
+
+def backward(proj, hat, kept, out_w, resid, conv_p, head_p, chan_p, gain, expand, seqs, heads):
     (cot_hi, cot_lo, conv, cum, step, state, mixed, cross, stat, edge) = kept
     tokens, pad = proj.shape
     chunk, width = resid.shape
@@ -1570,12 +1595,13 @@
             shape((tokens, pad), BF16),
             shape((tokens, pad), BF16),
             shape((chans, width), F32),
+            shape((chans, width), F32),
             shape((8, wide), F32),
             shape((8, chans), F32),
             shape((8, 128), F32),
         ),
-        in_specs=[anywhere] * 4 + [local] * 7 + [anywhere] + [local] * 5,
-        out_specs=(local, local, local, anywhere, local, local, local),
+        in_specs=[anywhere] * 7 + [local] * 6 + [anywhere] + [local] * 6,
+        out_specs=(local, local, local, anywhere, anywhere, local, local, local),
         scratch_shapes=[
             pltpu.VMEM((8 + tokens, pad), F32),
             pltpu.VMEM((tokens, chans), BF16),
@@ -1594,34 +1620,26 @@
             pltpu.VMEM((tokens, width // 2), BF16),
             pltpu.VMEM((tokens, width // 2), BF16),
             pltpu.VMEM((chans, width), F32),
-            pltpu.VMEM((half, width), F32),
-            pltpu.VMEM((half, width), F32),
-            pltpu.VMEM((rounds, half, width), F32),
+            pltpu.VMEM((tokens, 128), F32),
+            pltpu.VMEM((2, BLOCK, wide), F32),
             pltpu.VMEM((8, 128), F32),
-            sems((outs * (ins - 1),)),
-            sems((outs * (ins - 1),)),
-            sems((outs,)),
-            sems((outs + 1,)),
+            *seq_sum_scratch(half, width, rounds),
+            *seq_sum_scratch(half, width, rounds),
+            *line_reduce_sems(ins, outs),
             sems((5,)),
             sems((seqs - 1,)),
             sems((seqs - 1,)),
             sems,
             sems,
-            sems,
-            sems,
-            sems((rounds,)),
-            sems((rounds,)),
-            sems,
-            sems,
-            sems,
+            sems((2,)),
         ],
         compiler_params=pltpu.CompilerParams(
             collective_id=4, has_side_effects=True, vmem_limit_bytes=VMEM_LIMIT
         ),
         name="backward",
     )(
-        proj, edge, cot_hi, cot_lo, conv, cum, step, state, mixed, cross, stat,
-        out_w, resid, conv_p, head_p, chan_p, expand,
+        proj, edge, cot_hi, cot_lo, *hat, conv, cum, step, state, mixed, cross, stat,
+        out_w, resid, conv_p, head_p, chan_p, gain, expand,
     )
 
 
@@ -1683,8 +1701,28 @@
         heads,
     )
     kept = forward(projected, cot, out_weight, conv_p, head_p, chan_p, expand, seqs, heads)
-    result, grad_hi, grad_lo, out_weight_grad, wide_sums, chan_sums, head_sums = backward(
-        projected, kept, out_weight, resid, conv_p, head_p, chan_p, expand, seqs, heads
+    (
+        result,
+        grad_hi,
+        grad_lo,
+        out_weight_grad,
+        gate_weight_grad,
+        wide_sums,
+        chan_sums,
+        head_sums,
+    ) = backward(
+        projected,
+        (hat_hi, hat_lo),
+        kept,
+        out_weight,
+        resid,
+        conv_p,
+        head_p,
+        chan_p,
+        gain,
+        expand,
+        seqs,
+        heads,
     )
 
     def packed(*parts):
@@ -1708,7 +1746,7 @@
             eight(jnp.concatenate([jnp.zeros((1, width), F32), all_small], 0)),
         ]
     )
-    residual_grad, gate_weight_grad, inner_weight_grad, bc_pieces, sums = tail(
+    residual_grad, inner_weight_grad, bc_pieces, sums = tail(
         (grad_hi, grad_lo),
         (hat_hi, hat_lo),
         (weight_hi, weight_lo),

time: 442 us -> 398 us (0.900)
  the two profiles are of different devices: /device:TPU:0 before, /device:TPU:17 now
where the time goes in v2:
time: 398 us; the launch traced here: 391 us
  Pallas kernels  363 us (91%)
  local copies, waits for them, and re-layouts  24.6 us (6%)
    pallas_call x1, Pallas kernels, tail(): pl.pallas_call(functools.partial(tail_kernel, (seqs, heads, chunk, chans,...  103 us
    pallas_call x1, Pallas kernels, backward(): pl.pallas_call(functools.partial(backward_kernel, (seqs, heads, chunk, ch...  99.6 us
    pallas_call x1, Pallas kernels, forward(): pl.pallas_call(functools.partial(forward_kernel, (seqs, heads, chunk, cha...  84.1 us
    pallas_call x1, Pallas kernels, gather_project(): pl.pallas_call(functools.partial(head_kernel, (heads, chunk, chans, pad))...  75.8 us
    unnamed x32, local copies, waits for them, and re-layouts  12.5 us

profile of v2, /device:TPU:17, one launch (start us, length us, event | category | flops | bytes accessed | tf_op | source)
XLA Modules:
  0.0 391.3 jit_solution(9802477168416052996)
XLA Ops:
  0.6 1.3 reshape.75.refs_1_.refs_18_.refs_9_
  1.9 1.8 pad.36.refs_5_
  3.7 0.0 copy-start.10
  3.7 0.0 copy-start.8
  3.7 0.0 copy-start.12
  3.7 0.0 copy-start.11
  3.8 75.8 %gather_project.1 = (bf16[1024,1536]{1,0:T(8,128)(2,1)}, bf16[1024,1536]{1,0:T(8,128)(2,1)}, f32[1024,1152]{1,0:T(8,128)}, bf16[1152,1536]{1,0:T(8,128)(2,1)}, bf16[1152,1536]{1,0:T(8,128)(2,1)}) custom-call(f32[128,1536]{1,0:T(8,128)} %bitcast.24, f32[1,1536]{1,0:T(1,128)} %reshape.75.refs_1_.refs_18_.refs_9_, f32[384,1536]{1,0:T(8,128)} %refs_2_.2, ...), custom_call_target="tpu_custom_call" | custom-call | tf_op jit(solution)/shard_map/gather_project/pallas_call | solution.py:624
  79.6 0.7 fusion.refs_6_.refs_19_
  80.3 0.0 copy-done.7
  80.4 0.0 copy-done.5
  80.4 0.0 copy-done.6
  80.4 0.6 select_maximum_fusion.refs_3_.refs_15_
  81.0 0.0 copy-done.10
  81.0 0.1 broadcast_in_dim.8
  81.1 0.1 stack_reshape.3
  81.1 0.0 copy-done.8
  81.2 0.6 select_maximum_fusion.2.refs_5_.refs_17_
  81.8 0.0 copy-done.12
  81.8 0.1 pad.52.clone
  81.8 0.1 maximum_maximum_fusion
  81.9 0.6 pad.61.refs_4_.refs_16_
  82.5 84.1 %forward.1 = (bf16[1024,1536]{1,0:T(8,128)(2,1)}, bf16[1024,1536]{1,0:T(8,128)(2,1)}, f32[1024,640]{1,0:T(8,128)}, f32[1024,128]{1,0:T(8,128)}, f32[1024,128]{1,...) custom-call(f32[1024,1152]{1,0:T(8,128)} %get-tuple-element.43.refs_, ...), custom_call_target="tpu_custom_call" | custom-call | tf_op jit(solution)/shard_map/forward/pallas_call | solution.py:1031
  166.6 99.6 %backward.1 = (f32[128,1536]{1,0:T(8,128)}, bf16[1024,1152]{1,0:T(8,128)(2,1)}, bf16[1024,1152]{1,0:T(8,128)(2,1)}, f32[384,1536]{1,0:T(8,128)}, f32[384,1536]{1...) custom-call(f32[1024,1152]{1,0:T(8,128)} %get-tuple-element.43.refs_0_, ...), custom_call_target="tpu_custom_call" | custom-call | tf_op jit(solution)/shard_map/backward/pallas_call | solution.py:1591
  266.2 0.7 slice.80
  266.9 0.8 slice_reduce_fusion.2
  267.7 0.1 reshape_squeeze.7
  267.8 0.1 reduce_sum.9
  267.9 0.7 slice_reduce_fusion.4
  268.7 0.8 slice_bitcast_fusion.1
  269.4 0.1 concatenate.18
  269.5 0.7 slice.86
  270.3 0.7 pad_maximum_fusion.refs_6_
  271.0 103.1 %tail.1 = (f32[128,1536]{1,0:T(8,128)}, f32[384,1536]{1,0:T(8,128)}, f32[32,8,1536]{2,1,0:T(8,128)}, f32[3,8,1536]{2,1,0:T(8,128)}) custom-call(bf16[1024,1152]{1,0:T(8,128)(2,1)} %get-tuple-element.57.refs_0_, bf16[1024,1152]{1,0:T(8,128)(2,1)} %get-tuple-element.58.refs_1_, bf16[1024,1536]{1,0:T(8,128)(2,1)} %get-tuple-element.47.refs_4_.refs_2_, ...), custom_call_target="tpu_custom_call" | custom-call | tf_op jit(solution)/shard_map/tail/pallas_call | solution.py:398
  374.2 3.1 copy.33
  377.3 0.6 slice.102
  377.9 0.6 fusion.5
  378.5 0.6 fusion.6
  379.1 0.6 slice.103
  379.6 0.6 slice_bitcast_fusion
  380.3 0.6 slice_reduce_fusion
  380.9 0.6 reshape.85
  381.5 0.9 copy.39
  382.4 2.1 copy.40
  384.5 1.4 copy.41
  385.9 1.1 copy-done.2
  387.0 1.4 copy.42
  388.4 1.1 copy-done
  389.5 1.4 copy.43
  (33 shorter events, 0.2 us)
Async XLA Ops:
  3.7 76.6 %copy-start.7 = (f32[384]{0:T(512)S(1)}, f32[384]{0:T(512)}, u32[]{:S(2)}) copy-start(f32[384]{0:T(512)} %param.23) | copy-start | bytes 4612
  3.7 76.6 %copy-start.9 = (f32[256]{0:T(256)S(1)}, f32[256]{0:T(256)}, u32[]{:S(2)}) copy-start(f32[256]{0:T(256)} %param.25) | copy-start | bytes 3076
  3.7 76.7 %copy-start.5 = (f32[4,384]{1,0:T(4,128)S(1)}, f32[4,384]{1,0:T(4,128)}, u32[]{:S(2)}) copy-start(f32[4,384]{1,0:T(4,128)} %param.22) | copy-start | bytes 18436
  3.7 76.7 %copy-start.6 = (f32[4,256]{1,0:T(4,128)S(1)}, f32[4,256]{1,0:T(4,128)}, u32[]{:S(2)}) copy-start(f32[4,256]{1,0:T(4,128)} %param.24) | copy-start | bytes 12292
  3.7 77.3 %copy-start.10 = (f32[6]{0:T(128)S(1)}, f32[6]{0:T(128)}, u32[]{:S(2)}) copy-start(f32[6]{0:T(128)} %param.28) | copy-start | bytes 76
  3.7 77.4 %copy-start.8 = (f32[384]{0:T(512)S(1)}, f32[384]{0:T(512)}, u32[]{:S(2)}) copy-start(f32[384]{0:T(512)} %param.29) | copy-start | bytes 4612
  3.7 78.0 %copy-start.12 = (f32[6]{0:T(128)S(1)}, f32[6]{0:T(128)}, u32[]{:S(2)}) copy-start(f32[6]{0:T(128)} %param.27) | copy-start | bytes 76
  3.7 78.1 %copy-start.11 = (f32[6]{0:T(128)S(1)}, f32[6]{0:T(128)}, u32[]{:S(2)}) copy-start(f32[6]{0:T(128)} %param.26) | copy-start | bytes 76
  374.1 3.1 copy-start.4
  374.1 7.4 %copy-start.3 = (f32[128,1536]{1,0:T(8,128)S(1)}, f32[128,1536]{1,0:T(8,128)}, u32[]{:S(2)}) copy-start(f32[128,1536]{1,0:T(8,128)} %get-tuple-element.56) | copy-start | bytes 2359300
  377.3 7.2 %copy-start.1 = (f32[384,1536]{1,0:T(8,128)S(1)}, f32[384,1536]{1,0:T(8,128)}, u32[]{:S(2)}) copy-start(f32[384,1536]{1,0:T(8,128)} %get-tuple-element.136) | copy-start | bytes 7077892
  384.5 2.5 copy-start.2
  387.0 2.5 copy-start
